TPU v7x, 128 devices: a whole 4x4x4 slice. The times are simulated.
128 devices in a mesh: dp: 1, tp: 128 (over z, y, x, core).
Axes of the slice: x: 4, y: 4, z: 4, core: 2. Of those that a mesh axis runs over, the one named last changes fastest.
Arguments:
- x_rows: bfloat16 [4096, 16384], P(('dp', 'tp'))
- norm_gain: float32 [16384], replicated
- w_q: bfloat16 [16384, 128, 128], P(None, 'tp')
- w_k: bfloat16 [16384, 1024], P(None, 'tp')
- w_v: bfloat16 [16384, 1024], P(None, 'tp')
Outputs:
- output 1: bfloat16 [4096, 128, 128], P('dp', 'tp')
- output 2: bfloat16 [4096, 128, 128], P('dp', 'tp')
- output 3: bfloat16 [4096, 128, 128], P('dp', 'tp')
All inputs are finite; a program needn't handle non-finite values.
Results may differ from a plain program's by a relative error of at most 0.001.
Values are sent between devices in bfloat16 or wider.
A program may use at most 1 GiB of HBM per device.

v0:
```python
import jax
import jax.numpy as jnp
from jax import lax
from jax.sharding import PartitionSpec as P

EPSILON = 1e-6


def solution(mesh):
    group_size = mesh.shape["tp"]

    def head_pieces(piece, head_share):
        member = lax.axis_index("tp") % head_share
        received = [piece]
        for step_ahead in range(1, head_share):
            send_pairs = [(source, (source // head_share) * head_share + (source % head_share - step_ahead) % head_share) for source in range(group_size)]
            received.append(lax.ppermute(piece, "tp", send_pairs))
        joined = jnp.concatenate(received, axis=1)
        return jnp.roll(joined, member * piece.shape[1], axis=1)

    def local_step(x_rows, norm_gain, w_q, w_k, w_v):
        x_wide = x_rows.astype(jnp.float32)
        mean_sq = jnp.mean(x_wide * x_wide, axis=-1, keepdims=True)
        normed = (x_wide * lax.rsqrt(mean_sq + EPSILON) * norm_gain).astype(jnp.bfloat16)
        gathered = lax.all_gather(normed, "tp", axis=0, tiled=True)
        q_local = jnp.einsum("td,dhe->the", gathered, w_q, preferred_element_type=jnp.float32).astype(jnp.bfloat16)
        k_piece = jnp.dot(gathered, w_k, preferred_element_type=jnp.float32).astype(jnp.bfloat16)
        v_piece = jnp.dot(gathered, w_v, preferred_element_type=jnp.float32).astype(jnp.bfloat16)
        head_share = w_q.shape[2] // w_k.shape[1]
        k_head = head_pieces(k_piece, head_share)
        v_head = head_pieces(v_piece, head_share)
        return q_local, k_head[:, None, :], v_head[:, None, :]

    return jax.shard_map(local_step, mesh=mesh, in_specs=(P(("dp", "tp"), None), P(None), P(None, "tp", None), P(None, "tp"), P(None, "tp")), out_specs=(P("dp", "tp", None), P("dp", "tp", None), P("dp", "tp", None)), check_vma=False)
```

profile of v0, /device:TPU:1, one launch (start us, length us, event | category | flops | bytes accessed | tf_op | source)
XLA Modules:
  0.0 505.1 jit_solution(15504427204541769655)
XLA Ops:
  7.2 0.0 copy-start
  7.2 0.0 all-gather.2.cloned.1.call-start
  7.2 1.6 fusion.2
  8.8 2.5 fusion.4
  11.3 0.0 all-gather.2.cloned.1.call-update
  11.4 286.9 %all-gather.2.cloned.1.call-done = bf16[4096,16384]{1,0:T(8,128)(2,1)} async-done(((bf16[32,16384]{1,0:T(8,128)(2,1)}), bf16[4096,16384]{1,0:T(8,128)(2,1)}) %all-gather.2.cloned.1.call-update) | async-done | bytes 134217744 | tf_op jit(solution)/shard_map/all_gather | solution.py:25
  298.2 47.7 %constant_dynamic-update-slice_fusion.31 = (bf16[4096,128]{0,1:T(8,128)(2,1)S(1)}, bf16[4096,8]{0,1:T(8,128)(2,1)S(1)}) fusion(bf16[4096,16384]{1,0:T(8,128)(2,1)} %all-gather.2.cloned.1.call-done, bf16[16384,8]{0,1:T(8,128)(2,1)S(1)} %copy-done), kind=kOutput, calls=%fused_computation.47 | convolution fusion | flops 1073774592 | bytes 134610944 | tf_op jit(solution)/shard_map/dot_general | solution.py:28
  345.9 0.3 collective-permute-start.15
  346.2 3.3 collective-permute-start.16
  349.6 1.1 collective-permute-start.17
  350.7 2.4 collective-permute-start.18
  353.1 0.6 collective-permute-start.19
  353.7 48.8 %fusion = bf16[4096,1,128]{2,0,1:T(8,128)(2,1)} fusion(bf16[4096,16384]{1,0:T(8,128)(2,1)} %all-gather.2.cloned.1.call-done, bf16[16384,1,128]{2,0,1:T(8,128)(2,1)} %param.9), kind=kOutput, calls=%fused_computation.1 | convolution fusion | flops 17180393472 | bytes 139460608 | tf_op jit(solution)/shard_map/td,dhe->the/dot_general | solution.py:26
  402.5 47.7 %constant_dynamic-update-slice_fusion.15 = (bf16[4096,128]{0,1:T(8,128)(2,1)S(1)}, bf16[4096,8]{0,1:T(8,128)(2,1)S(1)}) fusion(bf16[4096,16384]{1,0:T(8,128)(2,1)} %all-gather.2.cloned.1.call-done, bf16[16384,8]{0,1:T(8,128)(2,1)S(1)} %copy-done.2), kind=kOutput, calls=%fused_computation.31 | convolution fusion | flops 1073774592 | bytes 134610944 | tf_op jit(solution)/shard_map/dot_general | solution.py:27
  450.2 0.0 collective-permute-done.15
  450.2 1.9 collective-permute-start.20
  452.1 0.0 collective-permute-done.16
  452.1 1.2 collective-permute-start.21
  453.3 0.0 collective-permute-done.17
  453.3 1.3 collective-permute-start.22
  454.5 0.0 collective-permute-done.18
  454.6 0.1 collective-permute-start.23
  454.7 0.0 collective-permute-done.19
  454.7 1.8 collective-permute-start.24
  456.5 0.0 collective-permute-done.20
  456.5 3.3 collective-permute-start.25
  459.8 0.0 collective-permute-done.21
  459.8 0.3 collective-permute-start.26
  460.1 0.0 collective-permute-done.22
  460.1 3.4 collective-permute-start.27
  463.5 0.0 collective-permute-done.23
  463.5 0.1 collective-permute-start.28
  463.6 0.1 collective-permute-start.29
  463.7 0.5 collective-permute-start
  464.3 2.2 collective-permute-done.26
  466.5 1.4 collective-permute-start.1
  467.9 0.0 collective-permute-done.27
  467.9 0.5 collective-permute-start.2
  468.4 0.5 collective-permute-done.28
  469.0 4.1 collective-permute-start.3
  473.1 0.2 collective-permute-start.4
  473.3 0.8 collective-permute-start.5
  474.2 0.0 collective-permute-done.1
  474.2 2.2 collective-permute-start.6
  476.4 0.1 collective-permute-start.7
  476.5 0.0 collective-permute-done.3
  476.5 1.7 collective-permute-start.8
  478.2 1.5 collective-permute-done.4
  479.7 0.0 collective-permute-start.9
  479.7 0.0 collective-permute-done.5
  479.7 2.5 collective-permute-start.10
  482.2 1.9 collective-permute-start.11
  484.2 0.0 collective-permute-done.7
  484.2 3.7 collective-permute-start.12
  487.9 0.1 collective-permute-start.13
  488.0 0.0 collective-permute-done.9
  488.0 0.1 collective-permute-start.14
  488.1 0.0 collective-permute-done.10
  488.1 0.4 collective-permute-done.11
  488.5 2.4 collective-permute-done.12
  490.9 2.3 collective-permute-done.13
  493.2 2.4 fusion.5
  495.6 1.3 copy.8
  496.9 1.3 copy.9
  (44 shorter events, 0.2 us)
Async XLA Ops:
  7.2 291.1 %copy-start = (bf16[16384,8]{0,1:T(8,128)(2,1)S(1)}, bf16[16384,8]{0,1:T(8,128)(2,1)}, u32[]{:S(2)}) copy-start(bf16[16384,8]{0,1:T(8,128)(2,1)} %param.11) | copy-start | bytes 786436
  7.2 291.0 %all-gather.2.cloned.1.call-start = ((), (), s32[]{:S(2)}) async-start(), calls=%async_computation | async-start | bytes 135266304 | tf_op jit(solution)/shard_map/all_gather | solution.py:25
  345.9 56.6 %copy-start.2 = (bf16[16384,8]{0,1:T(8,128)(2,1)S(1)}, bf16[16384,8]{0,1:T(8,128)(2,1)}, u32[]{:S(2)}) copy-start(bf16[16384,8]{0,1:T(8,128)(2,1)} %param.10) | copy-start | bytes 786436
  345.9 104.3 %collective-permute-start.15 = (bf16[4096,8]{0,1:T(8,128)(2,1)S(1)}, bf16[4096,8]{0,1:T(8,128)(2,1)S(1)}, u32[]{:S(2)}, u32[]{:S(2)}) collective-permute-start(bf16[4096,8]{0,1:T(8,128)(2,1)S(1)} %get-tuple-element.7), channel_id=1, source_target_pairs={{0,15},{1,0},{2,1},{3,2},{4,3},{5,4},{6,5},{7,6},{8,7},{9,8},{10,9... | collective-permute-start | bytes 196616 | tf_op jit(solution)/shard_map/ppermute | solution.py:17
  346.2 105.8 %collective-permute-start.16 = (bf16[4096,8]{0,1:T(8,128)(2,1)S(1)}, bf16[4096,8]{0,1:T(8,128)(2,1)S(1)}, u32[]{:S(2)}, u32[]{:S(2)}) collective-permute-start(bf16[4096,8]{0,1:T(8,128)(2,1)S(1)} %get-tuple-element.7), channel_id=1, source_target_pairs={{0,14},{1,15},{2,0},{3,1},{4,2},{5,3},{6,4},{7,5},{8,6},{9,7},{10,... | collective-permute-start | bytes 196616 | tf_op jit(solution)/shard_map/ppermute | solution.py:17
  349.6 103.7 %collective-permute-start.17 = (bf16[4096,8]{0,1:T(8,128)(2,1)S(1)}, bf16[4096,8]{0,1:T(8,128)(2,1)S(1)}, u32[]{:S(2)}, u32[]{:S(2)}) collective-permute-start(bf16[4096,8]{0,1:T(8,128)(2,1)S(1)} %get-tuple-element.7), channel_id=1, source_target_pairs={{0,13},{1,14},{2,15},{3,0},{4,1},{5,2},{6,3},{7,4},{8,5},{9,6},{10... | collective-permute-start | bytes 196616 | tf_op jit(solution)/shard_map/ppermute | solution.py:17
  350.7 103.8 %collective-permute-start.18 = (bf16[4096,8]{0,1:T(8,128)(2,1)S(1)}, bf16[4096,8]{0,1:T(8,128)(2,1)S(1)}, u32[]{:S(2)}, u32[]{:S(2)}) collective-permute-start(bf16[4096,8]{0,1:T(8,128)(2,1)S(1)} %get-tuple-element.7), channel_id=1, source_target_pairs={{0,12},{1,13},{2,14},{3,15},{4,0},{5,1},{6,2},{7,3},{8,4},{9,5},{1... | collective-permute-start | bytes 196616 | tf_op jit(solution)/shard_map/ppermute | solution.py:17
  353.1 101.6 %collective-permute-start.19 = (bf16[4096,8]{0,1:T(8,128)(2,1)S(1)}, bf16[4096,8]{0,1:T(8,128)(2,1)S(1)}, u32[]{:S(2)}, u32[]{:S(2)}) collective-permute-start(bf16[4096,8]{0,1:T(8,128)(2,1)S(1)} %get-tuple-element.7), channel_id=1, source_target_pairs={{0,11},{1,12},{2,13},{3,14},{4,15},{5,0},{6,1},{7,2},{8,3},{9,4},{... | collective-permute-start | bytes 196616 | tf_op jit(solution)/shard_map/ppermute | solution.py:17
  450.2 6.3 %collective-permute-start.20 = (bf16[4096,8]{0,1:T(8,128)(2,1)S(1)}, bf16[4096,8]{0,1:T(8,128)(2,1)S(1)}, u32[]{:S(2)}, u32[]{:S(2)}) collective-permute-start(bf16[4096,8]{0,1:T(8,128)(2,1)S(1)} %get-tuple-element.7), channel_id=1, source_target_pairs={{0,10},{1,11},{2,12},{3,13},{4,14},{5,15},{6,0},{7,1},{8,2},{9,3},... | collective-permute-start | bytes 196616 | tf_op jit(solution)/shard_map/ppermute | solution.py:17
  452.1 7.8 %collective-permute-start.21 = (bf16[4096,8]{0,1:T(8,128)(2,1)S(1)}, bf16[4096,8]{0,1:T(8,128)(2,1)S(1)}, u32[]{:S(2)}, u32[]{:S(2)}) collective-permute-start(bf16[4096,8]{0,1:T(8,128)(2,1)S(1)} %get-tuple-element.7), channel_id=1, source_target_pairs={{0,9},{1,10},{2,11},{3,12},{4,13},{5,14},{6,15},{7,0},{8,1},{9,2},... | collective-permute-start | bytes 196616 | tf_op jit(solution)/shard_map/ppermute | solution.py:17
  453.3 6.9 %collective-permute-start.22 = (bf16[4096,8]{0,1:T(8,128)(2,1)S(1)}, bf16[4096,8]{0,1:T(8,128)(2,1)S(1)}, u32[]{:S(2)}, u32[]{:S(2)}) collective-permute-start(bf16[4096,8]{0,1:T(8,128)(2,1)S(1)} %get-tuple-element.7), channel_id=1, source_target_pairs={{0,8},{1,9},{2,10},{3,11},{4,12},{5,13},{6,14},{7,15},{8,0},{9,1},... | collective-permute-start | bytes 196616 | tf_op jit(solution)/shard_map/ppermute | solution.py:17
  454.6 8.9 %collective-permute-start.23 = (bf16[4096,8]{0,1:T(8,128)(2,1)S(1)}, bf16[4096,8]{0,1:T(8,128)(2,1)S(1)}, u32[]{:S(2)}, u32[]{:S(2)}) collective-permute-start(bf16[4096,8]{0,1:T(8,128)(2,1)S(1)} %get-tuple-element.7), channel_id=1, source_target_pairs={{0,7},{1,8},{2,9},{3,10},{4,11},{5,12},{6,13},{7,14},{8,15},{9,0},... | collective-permute-start | bytes 196616 | tf_op jit(solution)/shard_map/ppermute | solution.py:17
  454.7 8.9 %collective-permute-start.24 = (bf16[4096,8]{0,1:T(8,128)(2,1)S(1)}, bf16[4096,8]{0,1:T(8,128)(2,1)S(1)}, u32[]{:S(2)}, u32[]{:S(2)}) collective-permute-start(bf16[4096,8]{0,1:T(8,128)(2,1)S(1)} %get-tuple-element.7), channel_id=1, source_target_pairs={{0,6},{1,7},{2,8},{3,9},{4,10},{5,11},{6,12},{7,13},{8,14},{9,15},... | collective-permute-start | bytes 196616 | tf_op jit(solution)/shard_map/ppermute | solution.py:17
  456.5 7.2 %collective-permute-start.25 = (bf16[4096,8]{0,1:T(8,128)(2,1)S(1)}, bf16[4096,8]{0,1:T(8,128)(2,1)S(1)}, u32[]{:S(2)}, u32[]{:S(2)}) collective-permute-start(bf16[4096,8]{0,1:T(8,128)(2,1)S(1)} %get-tuple-element.7), channel_id=1, source_target_pairs={{0,5},{1,6},{2,7},{3,8},{4,9},{5,10},{6,11},{7,12},{8,13},{9,14},{... | collective-permute-start | bytes 196616 | tf_op jit(solution)/shard_map/ppermute | solution.py:17
  459.8 6.6 %collective-permute-start.26 = (bf16[4096,8]{0,1:T(8,128)(2,1)S(1)}, bf16[4096,8]{0,1:T(8,128)(2,1)S(1)}, u32[]{:S(2)}, u32[]{:S(2)}) collective-permute-start(bf16[4096,8]{0,1:T(8,128)(2,1)S(1)} %get-tuple-element.7), channel_id=1, source_target_pairs={{0,4},{1,5},{2,6},{3,7},{4,8},{5,9},{6,10},{7,11},{8,12},{9,13},{1... | collective-permute-start | bytes 196616 | tf_op jit(solution)/shard_map/ppermute | solution.py:17
  460.1 7.8 %collective-permute-start.27 = (bf16[4096,8]{0,1:T(8,128)(2,1)S(1)}, bf16[4096,8]{0,1:T(8,128)(2,1)S(1)}, u32[]{:S(2)}, u32[]{:S(2)}) collective-permute-start(bf16[4096,8]{0,1:T(8,128)(2,1)S(1)} %get-tuple-element.7), channel_id=1, source_target_pairs={{0,3},{1,4},{2,5},{3,6},{4,7},{5,8},{6,9},{7,10},{8,11},{9,12},{10... | collective-permute-start | bytes 196616 | tf_op jit(solution)/shard_map/ppermute | solution.py:17
  463.5 5.5 %collective-permute-start.28 = (bf16[4096,8]{0,1:T(8,128)(2,1)S(1)}, bf16[4096,8]{0,1:T(8,128)(2,1)S(1)}, u32[]{:S(2)}, u32[]{:S(2)}) collective-permute-start(bf16[4096,8]{0,1:T(8,128)(2,1)S(1)} %get-tuple-element.7), channel_id=1, source_target_pairs={{0,2},{1,3},{2,4},{3,5},{4,6},{5,7},{6,8},{7,9},{8,10},{9,11},{10,... | collective-permute-start | bytes 196616 | tf_op jit(solution)/shard_map/ppermute | solution.py:17
  463.6 9.5 %collective-permute-start.29 = (bf16[4096,8]{0,1:T(8,128)(2,1)S(1)}, bf16[4096,8]{0,1:T(8,128)(2,1)S(1)}, u32[]{:S(2)}, u32[]{:S(2)}) collective-permute-start(bf16[4096,8]{0,1:T(8,128)(2,1)S(1)} %get-tuple-element.7), channel_id=1, source_target_pairs={{0,1},{1,2},{2,3},{3,4},{4,5},{5,6},{6,7},{7,8},{8,9},{9,10},{10,1... | collective-permute-start | bytes 196616 | tf_op jit(solution)/shard_map/ppermute | solution.py:17
  463.7 9.6 %collective-permute-start = (bf16[4096,8]{0,1:T(8,128)(2,1)S(1)}, bf16[4096,8]{0,1:T(8,128)(2,1)S(1)}, u32[]{:S(2)}, u32[]{:S(2)}) collective-permute-start(bf16[4096,8]{0,1:T(8,128)(2,1)S(1)} %get-tuple-element.5), channel_id=1, source_target_pairs={{0,15},{1,0},{2,1},{3,2},{4,3},{5,4},{6,5},{7,6},{8,7},{9,8},{10,9... | collective-permute-start | bytes 196616 | tf_op jit(solution)/shard_map/ppermute | solution.py:17
  466.5 7.7 %collective-permute-start.1 = (bf16[4096,8]{0,1:T(8,128)(2,1)S(1)}, bf16[4096,8]{0,1:T(8,128)(2,1)S(1)}, u32[]{:S(2)}, u32[]{:S(2)}) collective-permute-start(bf16[4096,8]{0,1:T(8,128)(2,1)S(1)} %get-tuple-element.5), channel_id=1, source_target_pairs={{0,14},{1,15},{2,0},{3,1},{4,2},{5,3},{6,4},{7,5},{8,6},{9,7},{10,... | collective-permute-start | bytes 196616 | tf_op jit(solution)/shard_map/ppermute | solution.py:17
  467.9 8.5 %collective-permute-start.2 = (bf16[4096,8]{0,1:T(8,128)(2,1)S(1)}, bf16[4096,8]{0,1:T(8,128)(2,1)S(1)}, u32[]{:S(2)}, u32[]{:S(2)}) collective-permute-start(bf16[4096,8]{0,1:T(8,128)(2,1)S(1)} %get-tuple-element.5), channel_id=1, source_target_pairs={{0,13},{1,14},{2,15},{3,0},{4,1},{5,2},{6,3},{7,4},{8,5},{9,6},{10... | collective-permute-start | bytes 196616 | tf_op jit(solution)/shard_map/ppermute | solution.py:17
  469.0 7.5 %collective-permute-start.3 = (bf16[4096,8]{0,1:T(8,128)(2,1)S(1)}, bf16[4096,8]{0,1:T(8,128)(2,1)S(1)}, u32[]{:S(2)}, u32[]{:S(2)}) collective-permute-start(bf16[4096,8]{0,1:T(8,128)(2,1)S(1)} %get-tuple-element.5), channel_id=1, source_target_pairs={{0,12},{1,13},{2,14},{3,15},{4,0},{5,1},{6,2},{7,3},{8,4},{9,5},{1... | collective-permute-start | bytes 196616 | tf_op jit(solution)/shard_map/ppermute | solution.py:17
  473.1 6.6 %collective-permute-start.4 = (bf16[4096,8]{0,1:T(8,128)(2,1)S(1)}, bf16[4096,8]{0,1:T(8,128)(2,1)S(1)}, u32[]{:S(2)}, u32[]{:S(2)}) collective-permute-start(bf16[4096,8]{0,1:T(8,128)(2,1)S(1)} %get-tuple-element.5), channel_id=1, source_target_pairs={{0,11},{1,12},{2,13},{3,14},{4,15},{5,0},{6,1},{7,2},{8,3},{9,4},{... | collective-permute-start | bytes 196616 | tf_op jit(solution)/shard_map/ppermute | solution.py:17
  473.3 19.9 %copy-start.1 = (bf16[4096,128]{0,1:T(8,128)(2,1)}, bf16[4096,128]{0,1:T(8,128)(2,1)S(1)}, u32[]{:S(2)}) copy-start(bf16[4096,128]{0,1:T(8,128)(2,1)S(1)} %constant_dynamic-update-slice_fusion.16) | copy-start | bytes 3145732
  473.3 6.4 %collective-permute-start.5 = (bf16[4096,8]{0,1:T(8,128)(2,1)S(1)}, bf16[4096,8]{0,1:T(8,128)(2,1)S(1)}, u32[]{:S(2)}, u32[]{:S(2)}) collective-permute-start(bf16[4096,8]{0,1:T(8,128)(2,1)S(1)} %get-tuple-element.5), channel_id=1, source_target_pairs={{0,10},{1,11},{2,12},{3,13},{4,14},{5,15},{6,0},{7,1},{8,2},{9,3},... | collective-permute-start | bytes 196616 | tf_op jit(solution)/shard_map/ppermute | solution.py:17
  474.2 8.1 %collective-permute-start.6 = (bf16[4096,8]{0,1:T(8,128)(2,1)S(1)}, bf16[4096,8]{0,1:T(8,128)(2,1)S(1)}, u32[]{:S(2)}, u32[]{:S(2)}) collective-permute-start(bf16[4096,8]{0,1:T(8,128)(2,1)S(1)} %get-tuple-element.5), channel_id=1, source_target_pairs={{0,9},{1,10},{2,11},{3,12},{4,13},{5,14},{6,15},{7,0},{8,1},{9,2},... | collective-permute-start | bytes 196616 | tf_op jit(solution)/shard_map/ppermute | solution.py:17
  476.4 7.8 %collective-permute-start.7 = (bf16[4096,8]{0,1:T(8,128)(2,1)S(1)}, bf16[4096,8]{0,1:T(8,128)(2,1)S(1)}, u32[]{:S(2)}, u32[]{:S(2)}) collective-permute-start(bf16[4096,8]{0,1:T(8,128)(2,1)S(1)} %get-tuple-element.5), channel_id=1, source_target_pairs={{0,8},{1,9},{2,10},{3,11},{4,12},{5,13},{6,14},{7,15},{8,0},{9,1},... | collective-permute-start | bytes 196616 | tf_op jit(solution)/shard_map/ppermute | solution.py:17
  476.5 11.3 %collective-permute-start.8 = (bf16[4096,8]{0,1:T(8,128)(2,1)S(1)}, bf16[4096,8]{0,1:T(8,128)(2,1)S(1)}, u32[]{:S(2)}, u32[]{:S(2)}) collective-permute-start(bf16[4096,8]{0,1:T(8,128)(2,1)S(1)} %get-tuple-element.5), channel_id=1, source_target_pairs={{0,7},{1,8},{2,9},{3,10},{4,11},{5,12},{6,13},{7,14},{8,15},{9,0},... | collective-permute-start | bytes 196616 | tf_op jit(solution)/shard_map/ppermute | solution.py:17
  479.7 8.3 %collective-permute-start.9 = (bf16[4096,8]{0,1:T(8,128)(2,1)S(1)}, bf16[4096,8]{0,1:T(8,128)(2,1)S(1)}, u32[]{:S(2)}, u32[]{:S(2)}) collective-permute-start(bf16[4096,8]{0,1:T(8,128)(2,1)S(1)} %get-tuple-element.5), channel_id=1, source_target_pairs={{0,6},{1,7},{2,8},{3,9},{4,10},{5,11},{6,12},{7,13},{8,14},{9,15},... | collective-permute-start | bytes 196616 | tf_op jit(solution)/shard_map/ppermute | solution.py:17
  479.7 8.3 %collective-permute-start.10 = (bf16[4096,8]{0,1:T(8,128)(2,1)S(1)}, bf16[4096,8]{0,1:T(8,128)(2,1)S(1)}, u32[]{:S(2)}, u32[]{:S(2)}) collective-permute-start(bf16[4096,8]{0,1:T(8,128)(2,1)S(1)} %get-tuple-element.5), channel_id=1, source_target_pairs={{0,5},{1,6},{2,7},{3,8},{4,9},{5,10},{6,11},{7,12},{8,13},{9,14},{... | collective-permute-start | bytes 196616 | tf_op jit(solution)/shard_map/ppermute | solution.py:17
  482.2 6.3 %collective-permute-start.11 = (bf16[4096,8]{0,1:T(8,128)(2,1)S(1)}, bf16[4096,8]{0,1:T(8,128)(2,1)S(1)}, u32[]{:S(2)}, u32[]{:S(2)}) collective-permute-start(bf16[4096,8]{0,1:T(8,128)(2,1)S(1)} %get-tuple-element.5), channel_id=1, source_target_pairs={{0,4},{1,5},{2,6},{3,7},{4,8},{5,9},{6,10},{7,11},{8,12},{9,13},{1... | collective-permute-start | bytes 196616 | tf_op jit(solution)/shard_map/ppermute | solution.py:17
  484.2 6.7 %collective-permute-start.12 = (bf16[4096,8]{0,1:T(8,128)(2,1)S(1)}, bf16[4096,8]{0,1:T(8,128)(2,1)S(1)}, u32[]{:S(2)}, u32[]{:S(2)}) collective-permute-start(bf16[4096,8]{0,1:T(8,128)(2,1)S(1)} %get-tuple-element.5), channel_id=1, source_target_pairs={{0,3},{1,4},{2,5},{3,6},{4,7},{5,8},{6,9},{7,10},{8,11},{9,12},{10... | collective-permute-start | bytes 196616 | tf_op jit(solution)/shard_map/ppermute | solution.py:17
  487.9 5.3 %collective-permute-start.13 = (bf16[4096,8]{0,1:T(8,128)(2,1)S(1)}, bf16[4096,8]{0,1:T(8,128)(2,1)S(1)}, u32[]{:S(2)}, u32[]{:S(2)}) collective-permute-start(bf16[4096,8]{0,1:T(8,128)(2,1)S(1)} %get-tuple-element.5), channel_id=1, source_target_pairs={{0,2},{1,3},{2,4},{3,5},{4,6},{5,7},{6,8},{7,9},{8,10},{9,11},{10,... | collective-permute-start | bytes 196616 | tf_op jit(solution)/shard_map/ppermute | solution.py:17
  488.0 5.2 %collective-permute-start.14 = (bf16[4096,8]{0,1:T(8,128)(2,1)S(1)}, bf16[4096,8]{0,1:T(8,128)(2,1)S(1)}, u32[]{:S(2)}, u32[]{:S(2)}) collective-permute-start(bf16[4096,8]{0,1:T(8,128)(2,1)S(1)} %get-tuple-element.5), channel_id=1, source_target_pairs={{0,1},{1,2},{2,3},{3,4},{4,5},{5,6},{6,7},{7,8},{8,9},{9,10},{10,1... | collective-permute-start | bytes 196616 | tf_op jit(solution)/shard_map/ppermute | solution.py:17
Sparse Core Ops, SparseCore 0:
  11.6 286.6 all-gather.1
where the time goes:
time: 505 us
  waiting for transfers between devices  296 us (59%)
  matrix products  144 us (29%)
  starting transfers between devices  41.1 us (8%)
  between operations  14.3 us (3%)
  other arithmetic  6.51 us (1%)
    all_gather x1, waiting for transfers between devices, local_step(): gathered = lax.all_gather(normed, 'tp', axis=0, tiled=True)  287 us
    dot_general x1, matrix products, local_step(): jnp.einsum('td,dhe->the', gathered, w_q, preferred_element_type=jnp.float32)  48.8 us
    dot_general x1, matrix products, local_step(): jnp.dot(gathered, w_v, preferred_element_type=jnp.float32)  47.7 us
    dot_general x1, matrix products, local_step(): jnp.dot(gathered, w_k, preferred_element_type=jnp.float32)  47.7 us
    ppermute x30, starting transfers between devices, head_pieces(): received.append(lax.ppermute(piece, 'tp', send_pairs))  41.1 us
  transfers between devices with their start and end apart: 31, of which 7 were waited for; matrix products, arithmetic and copies ran while one was open for 19% of the time, Pallas kernels for 0%

commit v1 on v0

v1 whole, which is shorter than its diff:
```python
import functools

import jax
import jax.numpy as jnp
from jax import lax
from jax.experimental import pallas as pl
from jax.experimental.pallas import tpu as pltpu
from jax.sharding import PartitionSpec as P

EPSILON = 1e-6
MESH = pl.DeviceIdType.MESH
DMA = pltpu.SemaphoreType.DMA


def rem(a, b):
    return lax.rem(a, b)


def kernel(
    depth, x_hbm, gain, wq_hbm, wkv_hbm, q_out, k_out, v_out,
    x_in, other, rows, wq, wkv, q_part, kv_part, q_got, kv_got, pieces, acc,
    load_sem, row_recv, wq_recv, wkv_recv, row_send, w_send, q_send, q_send_last, kv_send, q_recv, kv_recv,
    piece_send, piece_recv, pair_sem,
):
    half = depth // 2
    step = min(2048, half)
    steps = half // step
    me = lax.axis_index("tp")
    c = rem(me, 2)
    x = rem(me // 2, 4)
    y = rem(me // 8, 4)
    z = me // 32
    u = z + c * (y - z)
    v = y + c * (z - y)
    mate = me + 1 - 2 * c
    d = 1 - c

    def chip(xx, uu, vv):
        zz = uu + c * (vv - uu)
        yy = vv + c * (uu - vv)
        return ((zz * 4 + yy) * 4 + xx) * 2

    def plus(a, n):
        return rem(a + n, 4)

    def send(src, dst, send_sem, recv_sem, target):
        copy = pltpu.make_async_remote_copy(
            src_ref=src, dst_ref=dst, send_sem=send_sem, recv_sem=recv_sem, device_id={"tp": target}, device_id_type=MESH
        )
        copy.start()

    def got(ref, sem):
        pltpu.make_async_copy(ref, ref, sem).wait()

    load_x = pltpu.make_async_copy(x_hbm, x_in, load_sem.at[0])
    load_x.start()
    own_columns = pl.ds(pl.multiple_of(c * half, half), half)
    mate_columns = pl.ds(pl.multiple_of(d * half, half), half)
    load_wq = pltpu.make_async_copy(wq_hbm.at[own_columns, :], wq.at[u, c], load_sem.at[1])
    load_wq.start()
    load_wkv = pltpu.make_async_copy(wkv_hbm.at[:, own_columns], wkv.at[u, c], load_sem.at[2])
    load_wkv.start()

    barrier = pltpu.get_barrier_semaphore()
    y_pair = y + 1 - 2 * rem(y, 2)
    peers = [mate]
    for n in (1, 2, 3):
        for k in (0, 1):
            peers.append(((z * 4 + plus(y, n)) * 4 + x) * 2 + k)
            peers.append(((plus(z, n) * 4 + y) * 4 + x) * 2 + k)
        peers.append(((z * 4 + y) * 4 + plus(x, n)) * 2 + c)
        peers.append(((z * 4 + y_pair) * 4 + plus(x, n)) * 2 + c)
    for peer in peers:
        pl.semaphore_signal(barrier, inc=1, device_id={"tp": peer}, device_id_type=MESH)
    pl.semaphore_wait(barrier, len(peers))

    counts = {"row": 0, "w": 0}

    def send_row(xx, vv, k, target):
        send(rows.at[xx, vv, k], rows.at[xx, vv, k], row_send.at[counts["row"]], row_recv.at[xx, vv, k], target)
        counts["row"] += 1

    def row_got(xx, vv, k):
        got(rows.at[xx, vv, k], row_recv.at[xx, vv, k])

    def send_w(uu, k, target, q_src=None, kv_src=None, to=None):
        to = uu if to is None else to
        q_src = wq.at[uu, k] if q_src is None else q_src
        kv_src = wkv.at[uu, k] if kv_src is None else kv_src
        send(q_src, wq.at[to, k], w_send.at[counts["w"], 0], wq_recv.at[to, k], target)
        send(kv_src, wkv.at[to, k], w_send.at[counts["w"], 1], wkv_recv.at[to, k], target)
        counts["w"] += 1

    def w_got(uu, k):
        got(wq.at[uu, k], wq_recv.at[uu, k])
        got(wkv.at[uu, k], wkv_recv.at[uu, k])

    x_next, x_last = chip(plus(x, 1), u, v) + c, chip(plus(x, 3), u, v) + c
    v_next, v_last = chip(x, u, plus(v, 1)) + c, chip(x, u, plus(v, 3)) + c
    u_next, u_last = chip(x, plus(u, 1), v) + c, chip(x, plus(u, 3), v) + c

    send_w(u, c, mate, wq_hbm.at[mate_columns, :], wkv_hbm.at[:, mate_columns], to=v)
    send_w(u, c, u_next, wq_hbm.at[own_columns, :], wkv_hbm.at[:, own_columns])
    send_w(u, c, u_last, wq_hbm.at[own_columns, :], wkv_hbm.at[:, own_columns])

    load_x.wait()
    width = min(1024, half)

    def squares(j, total):
        part = x_in[:, pl.ds(pl.multiple_of(j * width, width), width)].astype(jnp.float32)
        return total + part * part

    total = lax.fori_loop(0, depth // width, squares, jnp.zeros((32, width), jnp.float32))
    scale = lax.rsqrt(jnp.sum(total, axis=1, keepdims=True) / depth + EPSILON)

    def normed(first):
        columns = pl.ds(pl.multiple_of(first, width), width)
        return (x_in[:, columns].astype(jnp.float32) * scale * gain[:, columns]).astype(jnp.bfloat16)

    @pl.loop(0, half // width)
    def _(j):
        columns = pl.ds(pl.multiple_of(j * width, width), width)
        other[:, columns] = normed(d * half + j * width)
        rows[x, v, c, :, columns] = normed(c * half + j * width)

    send(other, rows.at[x, u, c], row_send.at[counts["row"]], row_recv.at[x, u, c], mate)
    counts["row"] += 1
    for target in (x_next, x_last, v_next, v_last):
        send_row(x, v, c, target)
    row_got(x, v, d)
    for target in (x_next, x_last, v_next, v_last):
        send_row(x, v, d, target)
    w_got(u, d)
    send_w(u, d, u_next)
    send_w(u, d, u_last)

    row_got(x, plus(v, 3), c)
    send_row(x, plus(v, 3), c, v_next)
    row_got(plus(x, 3), v, c)
    send_row(plus(x, 3), v, c, x_next)
    row_got(x, plus(v, 1), c)
    for near in (3, 1):
        send_row(x, plus(v, near), c, x_next)
        send_row(x, plus(v, near), c, x_last)
    row_got(x, plus(v, 1), d)
    send_row(x, plus(v, 1), d, v_last)
    row_got(plus(x, 1), v, d)
    send_row(plus(x, 1), v, d, x_last)
    row_got(x, plus(v, 3), d)
    for near in (3, 1):
        send_row(x, plus(v, near), d, x_next)
        send_row(x, plus(v, near), d, x_last)
    for k in (c, d):
        row_got(x, plus(v, 2), k)
        send_row(x, plus(v, 2), k, x_next)
        send_row(x, plus(v, 2), k, x_last)

    def forward_x(vv):
        row_got(plus(x, 3), vv, c)
        send_row(plus(x, 3), vv, c, x_next)
        row_got(plus(x, 1), vv, d)
        send_row(plus(x, 1), vv, d, x_last)

    w_got(plus(u, 3), c)
    send_w(plus(u, 3), c, u_next)
    forward_x(plus(v, 3))
    w_got(plus(u, 1), d)
    send_w(plus(u, 1), d, u_last)
    forward_x(plus(v, 1))
    forward_x(plus(v, 2))
    for n in range(4):
        row_got(plus(x, 3), plus(v, n), d)
        row_got(plus(x, 1), plus(v, n), c)
    load_wq.wait()
    load_wkv.wait()
    w_got(plus(u, 3), d)
    w_got(plus(u, 1), c)
    w_got(plus(u, 2), c)
    w_got(plus(u, 2), d)

    def depth_slice(j):
        return pl.ds(pl.multiple_of(j * step, step), step)

    def q_product(load_rows, count, store):
        @pl.loop(0, 4)
        def _(uu):
            @pl.loop(0, steps)
            def _(j):
                right = jnp.concatenate([wq[uu, 0, depth_slice(j), :], wq[uu, 1, depth_slice(j), :]], axis=1)
                term = jnp.dot(load_rows(j), right, preferred_element_type=jnp.float32)

                @pl.when(j == 0)
                def _():
                    acc[pl.ds(0, count), :] = term

                @pl.when(j > 0)
                def _():
                    acc[pl.ds(0, count), :] += term

            for k in (0, 1):
                store(uu, k, acc[pl.ds(0, count), pl.ds(k * 128, 128)])

    targets = []
    for du in range(4):
        for dk in (0, 1):
            if du or dk:
                targets.append((plus(u, du), rem(c + dk, 2)))

    @pl.loop(0, 3)
    def _(g):
        xx = plus(x, g + g // 2)

        def store(uu, k, value):
            q_part[xx, uu, k] = value.reshape(4, 64, 128)

        q_product(lambda j: rows[xx, :, :, :, depth_slice(j)].reshape(256, step), 256, store)
        for n, (uu, k) in enumerate(targets):
            send(q_part.at[xx, uu, k], q_got.at[c, u, xx], q_send.at[g, n], q_recv.at[c, u], chip(x, uu, v) + k)

    far = plus(x, 2)

    @pl.loop(0, 4)
    def _(t):
        vv = plus(v, t + (t // 2) * (1 - 2 * (t // 3)))
        row_got(far, vv, c)
        row_got(far, vv, d)

        def store(uu, k, value):
            q_part[far, uu, k, vv] = value

        q_product(lambda j: rows[far, vv, :, :, depth_slice(j)].reshape(64, step), 64, store)
        for n, (uu, k) in enumerate(targets):
            send(q_part.at[far, uu, k, vv], q_got.at[c, u, far, vv], q_send_last.at[t, n], q_recv.at[c, u], chip(x, uu, v) + k)

        @pl.loop(0, steps)
        def _(j):
            term = lax.dot_general(
                wkv[:, :, :, depth_slice(j)].reshape(128, step),
                rows[:, vv, :, :, depth_slice(j)].reshape(256, step),
                (((1,), (1,)), ((), ())),
                preferred_element_type=jnp.float32,
            )

            @pl.when(j == 0)
            def _():
                acc[pl.ds(0, 128), :] = term

            @pl.when(j > 0)
            def _():
                acc[pl.ds(0, 128), :] += term

        kv_part[vv] = acc[pl.ds(0, 128), :].reshape(4, 2, 16, 256)
        for n, (uu, k) in enumerate(targets):
            send(kv_part.at[vv, uu, k], kv_got.at[c, u, vv], kv_send.at[t, n], kv_recv.at[c, u], chip(x, uu, v) + k)

    for n in range(4):
        q_got[c, u, n] = q_part[n, u, c]
        kv_got[c, u, n] = kv_part[n, u, c]
    for n in (1, 2, 3):
        got(kv_got.at[c, plus(u, n)], kv_recv.at[c, plus(u, n)])
    for n in range(4):
        got(kv_got.at[d, n], kv_recv.at[d, n])

    place = rem(y, 2) * 4 + x
    for zz in range(4):
        for yy in range(4):
            pieces[c, place, :, pl.ds((zz * 4 + yy) * 256, 256)] = (kv_got[0, zz, yy] + kv_got[1, yy, zz]).astype(jnp.bfloat16)
    for n in range(1, 8):
        there = rem(place + n, 8)
        target = ((z * 4 + (y // 2) * 2 + there // 4) * 4 + rem(there, 4)) * 2 + c
        send(pieces.at[c, place], pieces.at[c, place], piece_send.at[n], piece_recv.at[place], target)

    for n in (1, 2, 3):
        got(q_got.at[c, plus(u, n)], q_recv.at[c, plus(u, n)])
    for n in range(4):
        got(q_got.at[d, n], q_recv.at[d, n])

    @pl.loop(0, 4)
    def _(zz):
        @pl.loop(0, 4)
        def _(yy):
            for xx in range(4):
                q_out[zz, yy, xx] = (q_got[0, zz, xx, yy] + q_got[1, yy, xx, zz]).astype(jnp.bfloat16)

    for n in range(1, 8):
        there = rem(place + n, 8)
        got(pieces.at[c, there], piece_recv.at[there])
    pair = pltpu.make_async_remote_copy(
        src_ref=pieces.at[c], dst_ref=pieces.at[c], send_sem=pair_sem.at[0], recv_sem=pair_sem.at[1],
        device_id={"tp": mate}, device_id_type=MESH,
    )
    pair.start()
    got(pieces.at[d], pair_sem.at[1])

    @pl.loop(0, 16)
    def _(b):
        columns = pl.ds(pl.multiple_of(b * 256, 256), 256)
        wide = [pieces[k, n, :, columns].astype(jnp.float32) for n in range(8) for k in (0, 1)]
        out_rows = pl.ds(pl.multiple_of(b * 256, 256), 256)
        k_out[out_rows, :] = jnp.concatenate([w[0:8] for w in wide], axis=0).T.astype(jnp.bfloat16)
        v_out[out_rows, :] = jnp.concatenate([w[8:16] for w in wide], axis=0).T.astype(jnp.bfloat16)

    def left(ref, sem):
        pltpu.make_async_copy(ref, ref, sem).wait()

    for n in range(counts["row"]):
        left(rows.at[0, 0, 0], row_send.at[n])
    for n in range(counts["w"]):
        left(wq.at[0, 0], w_send.at[n, 0])
        left(wkv.at[0, 0], w_send.at[n, 1])
    for n in range(len(targets)):
        for g in range(3):
            left(q_part.at[0, 0, 0], q_send.at[g, n])
        for t in range(4):
            left(q_part.at[0, 0, 0, 0], q_send_last.at[t, n])
            left(kv_part.at[0, 0, 0], kv_send.at[t, n])
    for n in range(1, 8):
        left(pieces.at[0, 0], piece_send.at[n])
    left(pieces.at[0], pair_sem.at[0])


def solution(mesh):
    def local_step(x_rows, norm_gain, w_q, w_k, w_v):
        depth = x_rows.shape[1]
        half = depth // 2
        gain = norm_gain.reshape(1, depth)
        wq = w_q.reshape(depth, 128)
        wkv = jnp.concatenate([w_k.T, w_v.T], axis=0)
        any_space = pl.BlockSpec(memory_space=pl.ANY)
        vmem = pl.BlockSpec(memory_space=pltpu.VMEM)
        bf16, f32 = jnp.bfloat16, jnp.float32
        q, k, v = pl.pallas_call(
            functools.partial(kernel, depth),
            out_shape=(
                jax.ShapeDtypeStruct((4, 4, 4, 64, 128), bf16),
                jax.ShapeDtypeStruct((4096, 128), bf16),
                jax.ShapeDtypeStruct((4096, 128), bf16),
            ),
            in_specs=[any_space, vmem, any_space, any_space],
            out_specs=(vmem, vmem, vmem),
            scratch_shapes=[
                pltpu.VMEM((32, depth), bf16),
                pltpu.VMEM((32, half), bf16),
                pltpu.VMEM((4, 4, 2, 32, half), bf16),
                pltpu.VMEM((4, 2, half, 128), bf16),
                pltpu.VMEM((4, 2, 16, half), bf16),
                pltpu.VMEM((4, 4, 2, 4, 64, 128), f32),
                pltpu.VMEM((4, 4, 2, 16, 256), f32),
                pltpu.VMEM((2, 4, 4, 4, 64, 128), f32),
                pltpu.VMEM((2, 4, 4, 16, 256), f32),
                pltpu.VMEM((2, 8, 16, 4096), bf16),
                pltpu.VMEM((256, 256), f32),
                DMA((3,)),
                DMA((4, 4, 2)),
                DMA((4, 2)),
                DMA((4, 2)),
                DMA((31,)),
                DMA((7, 2)),
                DMA((3, 7)),
                DMA((4, 7)),
                DMA((4, 7)),
                DMA((2, 4)),
                DMA((2, 4)),
                DMA((8,)),
                DMA((8,)),
                DMA((2,)),
            ],
            compiler_params=pltpu.CompilerParams(collective_id=0, has_side_effects=True, vmem_limit_bytes=67043328),
        )(x_rows, gain, wq, wkv)
        return q.reshape(4096, 1, 128), k[:, None, :], v[:, None, :]

    return jax.shard_map(
        local_step,
        mesh=mesh,
        in_specs=(P(("dp", "tp"), None), P(None), P(None, "tp", None), P(None, "tp"), P(None, "tp")),
        out_specs=(P("dp", "tp", None), P("dp", "tp", None), P("dp", "tp", None)),
        check_vma=False,
    )
```

time: 505 us -> 202 us (0.40)
  waiting for transfers between devices: 296 us -> 0 us
  Pallas kernels: 0 us -> 194 us
  matrix products: 144 us -> 0 us
  starting transfers between devices: 41.1 us -> 0 us
  between operations: 14.3 us -> 0.65 us
    all_gather x1 -> x0, waiting for transfers between devices: 287 us -> none  [local_step(): gathered = lax.all_gather(normed, 'tp', axis=0, tiled=True)]
    pallas_call x0 -> x1, Pallas kernels: none -> 194 us  [local_step(): pl.pallas_call(functools.partial(kernel, depth), out_shape=(jax.ShapeDtyp...]
    dot_general x3 -> x0, matrix products: 144 us -> none  [the longest x1 48.8 us: local_step(): jnp.einsum('td,dhe->the', gathered, w_q, preferred_element_type=jnp.float32)]
    ppermute x30 -> x0, starting transfers between devices: 41.1 us -> none  [head_pieces(): received.append(lax.ppermute(piece, 'tp', send_pairs))]
    ppermute x30 -> x0, waiting for transfers between devices: 9.32 us -> none  [head_pieces(): received.append(lax.ppermute(piece, 'tp', send_pairs))]
    unnamed x34 -> x5, local copies, waits for them, and re-layouts: 0.17 us -> 5.59 us
  transfers between devices with their start and end apart: 31 -> 0, of which waited for: 7 -> 0; matrix products, arithmetic and copies ran while one was open for 19% -> 0% of each run, Pallas kernels for 0% -> 0%
where the time goes in v1:
time: 202 us
  Pallas kernels  194 us (96%)
  local copies, waits for them, and re-layouts  5.59 us (3%)
    pallas_call x1, Pallas kernels, local_step(): pl.pallas_call(functools.partial(kernel, depth), out_shape=(jax.ShapeDtyp...  194 us
    unnamed x5, local copies, waits for them, and re-layouts  5.59 us

profile of v1, /device:TPU:1, one launch (start us, length us, event | category | flops | bytes accessed | tf_op | source)
XLA Modules:
  0.0 202.0 jit_solution(7730896146412821994)
XLA Ops:
  0.6 1.9 pad_maximum_fusion.wkv_hbm
  2.5 193.9 %shard_map.76 = (bf16[4,4,4,64,128]{4,3,2,1,0:T(8,128)(2,1)}, bf16[4096,128]{1,0:T(8,128)(2,1)}, bf16[4096,128]{1,0:T(8,128)(2,1)}) custom-call(bf16[32,16384]{1,0:T(8,128)(2,1)} %x_hbm.1, f32[1,16384]{1,0:T(1,128)} %bitcast.13, bf16[16384,128]{1,0:T(8,128)(2,1)} %bitcast.7, bf16[16,16384]{1,0:T(8,128)(2,1)} %pad_maximum_fusion.wkv_hbm), custom_call_target="tpu_custom_call" | custom-call | tf_op jit(solution)/shard_map/pallas_call | solution.py:332
  196.4 0.0 copy-start
  196.4 2.4 %copy.11 = bf16[4096,1,128]{2,0,1:T(8,128)(2,1)} copy(bf16[4096,1,128]{2,0,1:T(8,128)(2,1)} %bitcast.10) | data formatting | bytes 2097152
  198.7 2.3 %copy.12 = bf16[4096,1,128]{2,0,1:T(8,128)(2,1)} copy(bf16[4096,1,128]{2,0,1:T(8,128)(2,1)} %bitcast.9) | data formatting | bytes 2097152
  201.0 0.0 copy-done
  201.0 1.0 copy.13
Async XLA Ops:
  196.4 4.6 %copy-start = (bf16[4096,128]{1,0:T(8,128)(2,1)S(1)}, bf16[4096,128]{1,0:T(8,128)(2,1)}, u32[]{:S(2)}) copy-start(bf16[4096,128]{1,0:T(8,128)(2,1)} %get-tuple-element.8) | copy-start | bytes 3145732

commit v2 on v0

v2 whole, which is shorter than its diff:
```python
import functools

import jax
import jax.numpy as jnp
from jax import lax
from jax.experimental import pallas as pl
from jax.experimental.pallas import tpu as pltpu
from jax.sharding import PartitionSpec as P

EPSILON = 1e-6
MESH = pl.DeviceIdType.MESH
DMA = pltpu.SemaphoreType.DMA


def rem(a, b):
    return lax.rem(a, b)


def kernel(
    depth, split, x_hbm, gain, wq_hbm, wk_hbm, wv_hbm, q_out, k_out, v_out,
    x_in, other, wkv_other, rows, wq, wkv, q_part, kv_part, q_got, kv_got, pieces,
    load_sem, wide_recv, thin_recv, row_send, wq_recv, wkv_recv, w_send, q_send, q_send_far, kv_send, q_recv, kv_recv,
    piece_send, piece_recv, pair_send, pair_recv,
):
    half = depth // 2
    me = lax.axis_index("tp")
    c = rem(me, 2)
    x = rem(me // 2, 4)
    y = rem(me // 8, 4)
    z = me // 32
    u = z + c * (y - z)
    v = y + c * (z - y)
    mate = me + 1 - 2 * c
    d = 1 - c

    def chip(xx, uu, vv):
        zz = uu + c * (vv - uu)
        yy = vv + c * (uu - vv)
        return ((zz * 4 + yy) * 4 + xx) * 2

    def plus(a, n):
        return rem(a + n, 4)

    def send(src, dst, send_sem, recv_sem, target):
        copy = pltpu.make_async_remote_copy(
            src_ref=src, dst_ref=dst, send_sem=send_sem, recv_sem=recv_sem, device_id={"tp": target}, device_id_type=MESH
        )
        copy.start()

    def got(ref, sem):
        pltpu.make_async_copy(ref, ref, sem).wait()

    load_x = pltpu.make_async_copy(x_hbm, x_in, load_sem.at[0])
    load_x.start()
    own_columns = pl.ds(pl.multiple_of(c * half, half), half)
    mate_columns = pl.ds(pl.multiple_of(d * half, half), half)
    loads = [
        pltpu.make_async_copy(wk_hbm.at[:, mate_columns], wkv_other.at[0:8], load_sem.at[1]),
        pltpu.make_async_copy(wv_hbm.at[:, mate_columns], wkv_other.at[8:16], load_sem.at[2]),
        pltpu.make_async_copy(wk_hbm.at[:, own_columns], wkv.at[u, c, 0:8], load_sem.at[3]),
        pltpu.make_async_copy(wv_hbm.at[:, own_columns], wkv.at[u, c, 8:16], load_sem.at[4]),
    ]
    for load in loads:
        load.start()
    load_wq = pltpu.make_async_copy(wq_hbm.at[own_columns, :], wq.at[u, c], load_sem.at[5])
    load_wq.start()

    barrier = pltpu.get_barrier_semaphore()
    y_pair = y + 1 - 2 * rem(y, 2)
    peers = [mate]
    for n in (1, 2, 3):
        for k in (0, 1):
            peers.append(((z * 4 + plus(y, n)) * 4 + x) * 2 + k)
            peers.append(((plus(z, n) * 4 + y) * 4 + x) * 2 + k)
        peers.append(((z * 4 + y) * 4 + plus(x, n)) * 2 + c)
        peers.append(((z * 4 + y_pair) * 4 + plus(x, n)) * 2 + c)
    for peer in peers:
        pl.semaphore_signal(barrier, inc=1, device_id={"tp": peer}, device_id_type=MESH)

    load_x.wait()
    width = min(1024, half)

    def squares(j, total):
        part = x_in[:, pl.ds(pl.multiple_of(j * width, width), width)].astype(jnp.float32)
        return total + part * part

    total = lax.fori_loop(0, depth // width, squares, jnp.zeros((32, width), jnp.float32))
    scale = lax.rsqrt(jnp.sum(total, axis=1, keepdims=True) / depth + EPSILON)

    def normed(first):
        columns = pl.ds(pl.multiple_of(first, width), width)
        return (x_in[:, columns].astype(jnp.float32) * scale * gain[:, columns]).astype(jnp.bfloat16)

    @pl.loop(0, half // width)
    def _(j):
        columns = pl.ds(pl.multiple_of(j * width, width), width)
        other[:, columns] = normed(d * half + j * width)
        rows[x, v, c, :, columns] = normed(c * half + j * width)

    for load in loads:
        load.wait()
    pl.semaphore_wait(barrier, len(peers))

    counts = {"row": 0, "w": 0, "kinds": []}
    wide, thin = slice(0, split), slice(split, half)

    def row_sem():
        counts["row"] += 1
        return row_send.at[counts["row"] - 1]

    def send_wide(xx, vv, k, *to):
        for target in to:
            send(rows.at[xx, vv, k, :, wide], rows.at[xx, vv, k, :, wide], row_sem(), wide_recv.at[xx, vv, k], target)
            counts["kinds"].append(wide)

    def send_thin(xx, vv, k, *to):
        for target in to:
            send(rows.at[xx, vv, k, :, thin], rows.at[xx, vv, k, :, thin], row_sem(), thin_recv.at[xx, vv, k], target)
            counts["kinds"].append(thin)

    def wide_got(xx, vv, k):
        got(rows.at[xx, vv, k, :, wide], wide_recv.at[xx, vv, k])

    def thin_got(xx, vv, k):
        got(rows.at[xx, vv, k, :, thin], thin_recv.at[xx, vv, k])

    def send_w(q_src, kv_src, uu, k, target):
        send(q_src, wq.at[uu, k], w_send.at[counts["w"], 0], wq_recv.at[uu, k], target)
        send(kv_src, wkv.at[uu, k], w_send.at[counts["w"], 1], wkv_recv.at[uu, k], target)
        counts["w"] += 1

    def pass_w(uu, k, target):
        send_w(wq.at[uu, k], wkv.at[uu, k], uu, k, target)

    def w_got(uu, k):
        got(wq.at[uu, k], wq_recv.at[uu, k])
        got(wkv.at[uu, k], wkv_recv.at[uu, k])

    x_next, x_last = chip(plus(x, 1), u, v) + c, chip(plus(x, 3), u, v) + c
    v_next, v_last = chip(x, u, plus(v, 1)) + c, chip(x, u, plus(v, 3)) + c
    u_next, u_last = chip(x, plus(u, 1), v) + c, chip(x, plus(u, 3), v) + c
    xp, xm, xo = plus(x, 1), plus(x, 3), plus(x, 2)
    vp, vm, vo = plus(v, 1), plus(v, 3), plus(v, 2)
    up, um, uo = plus(u, 1), plus(u, 3), plus(u, 2)

    send(other, rows.at[x, u, c], row_sem(), wide_recv.at[x, u, c], mate)
    send_thin(x, v, c, x_next, x_last)
    send_wide(x, v, c, v_next, v_last)
    send_w(wq_hbm.at[own_columns, :], wkv.at[u, c], u, c, u_next)
    send_w(wq_hbm.at[own_columns, :], wkv.at[u, c], u, c, u_last)
    send_w(wq_hbm.at[mate_columns, :], wkv_other, v, c, mate)
    got(rows.at[x, v, d], wide_recv.at[x, v, d])
    send_thin(x, v, d, x_next, x_last)
    send_wide(x, v, c, x_next, x_last)
    send_wide(x, v, d, x_next, x_last, v_next, v_last)
    for k in (c, d):
        send_thin(x, v, k, v_next, v_last)
    w_got(u, d)
    pass_w(u, d, u_next)
    pass_w(u, d, u_last)

    thin_got(xm, v, c)
    send_thin(xm, v, c, x_next)
    thin_got(xp, v, d)
    send_thin(xp, v, d, x_last)
    thin_got(xm, v, d)
    thin_got(xp, v, c)
    for xx in (xm, xp):
        for k in (c, d):
            send_thin(xx, v, k, v_next, v_last)

    wide_got(x, vm, c)
    send_wide(x, vm, c, v_next)
    wide_got(xm, v, c)
    send_wide(xm, v, c, x_next)
    wide_got(x, vp, c)
    for vv in (vm, vp):
        send_wide(x, vv, c, x_next, x_last)
    wide_got(x, vp, d)
    send_wide(x, vp, d, v_last)
    wide_got(xp, v, d)
    send_wide(xp, v, d, x_last)
    wide_got(x, vm, d)
    for vv in (vm, vp):
        send_wide(x, vv, d, x_next, x_last)
    for k in (c, d):
        thin_got(xo, v, k)
        send_thin(xo, v, k, v_next, v_last)
    for k in (c, d):
        wide_got(x, vo, k)
        send_wide(x, vo, k, x_next, x_last)
    for xx in (x, xm, xp, xo):
        thin_got(xx, vm, c)
        send_thin(xx, vm, c, v_next)
        thin_got(xx, vp, d)
        send_thin(xx, vp, d, v_last)

    def forward_x(vv):
        wide_got(xm, vv, c)
        send_wide(xm, vv, c, x_next)
        wide_got(xp, vv, d)
        send_wide(xp, vv, d, x_last)

    targets = []
    for du in range(4):
        for dk in (0, 1):
            if du or dk:
                targets.append((plus(u, du), rem(c + dk, 2)))

    def q_block(xx, uu):
        right = jnp.concatenate([wq[uu, 0], wq[uu, 1]], axis=1)
        value = jnp.dot(rows[xx].reshape(256, half), right, preferred_element_type=jnp.float32)
        for k in (0, 1):
            q_part[xx, uu, k] = value[:, k * 128:(k + 1) * 128].reshape(4, 64, 128)

    def kv_block(xx):
        value = lax.dot_general(
            wkv[...].reshape(128, half), rows[xx].reshape(256, half), (((1,), (1,)), ((), ())), preferred_element_type=jnp.float32
        )
        kv_part[xx] = value.reshape(4, 2, 16, 256)

    def send_q(g, xx):
        for n, (uu, k) in enumerate(targets):
            send(q_part.at[xx, uu, k], q_got.at[c, u, xx], q_send.at[g, n], q_recv.at[c, u, xx], chip(x, uu, v) + k)
        q_got[c, u, xx] = q_part[xx, u, c]

    def send_kv(g, xx):
        for n, (uu, k) in enumerate(targets):
            send(kv_part.at[xx, uu, k], kv_got.at[c, u, xx], kv_send.at[g, n], kv_recv.at[c, u, xx], chip(x, uu, v) + k)
        kv_got[c, u, xx] = kv_part[xx, u, c]

    senders = [(c, plus(u, n)) for n in (1, 2, 3)] + [(d, n) for n in range(4)]
    place = rem(y, 2) * 4 + x

    def add_kv(g, xx):
        for role, n in senders:
            got(kv_got.at[role, n, xx], kv_recv.at[role, n, xx])
        for zz in range(4):
            second = jnp.concatenate([kv_got[1, yy, xx][:, zz * 64:(zz + 1) * 64] for yy in range(4)], axis=1)
            pieces[c, g, place, :, pl.ds(zz * 256, 256)] = (kv_got[0, zz, xx] + second).astype(jnp.bfloat16)
        for n in range(1, 8):
            there = rem(place + n, 8)
            target = ((z * 4 + (y // 2) * 2 + there // 4) * 4 + rem(there, 4)) * 2 + c
            send(pieces.at[c, g, place], pieces.at[c, g, place], piece_send.at[g, n], piece_recv.at[g, place], target)

    def add_q(xx):
        for role, n in senders:
            got(q_got.at[role, n, xx], q_recv.at[role, n, xx])

        @pl.loop(0, 4)
        def _(zz):
            for yy in range(4):
                q_out[zz, yy, xx] = (q_got[0, zz, xx, yy] + q_got[1, yy, xx, zz]).astype(jnp.bfloat16)

    def share_kv(g):
        for n in range(1, 8):
            there = rem(place + n, 8)
            got(pieces.at[c, g, there], piece_recv.at[g, there])
        send(pieces.at[c, g], pieces.at[c, g], pair_send.at[g], pair_recv.at[g], mate)

    def finish_kv():
        for g in range(4):
            got(pieces.at[d, g], pair_recv.at[g])

        @pl.loop(0, 4)
        def _(zz):
            columns = pl.ds(pl.multiple_of(zz * 256, 256), 256)
            for xx in range(4):
                places = [((0, 2, 3, 1)[(xx - n) % 4], n) for n in range(8)]
                wide_pieces = [pieces[k, g, n, :, columns].astype(jnp.float32) for g, n in places for k in (0, 1)]
                for out, first in ((k_out, 0), (v_out, 8)):
                    value = jnp.concatenate([w[first:first + 8] for w in wide_pieces], axis=0).T.astype(jnp.bfloat16)
                    out[zz, :, xx] = value.reshape(4, 64, 128)

    w_got(um, c)
    pass_w(um, c, u_next)
    forward_x(vm)
    load_wq.wait()
    for k in (c, d):
        thin_got(x, vo, k)
    for vv, k in ((vm, d), (vp, c)):
        thin_got(x, vv, k)
    q_block(x, u)
    w_got(up, d)
    pass_w(up, d, u_last)
    forward_x(vp)
    w_got(um, d)
    w_got(up, c)
    q_block(x, um)
    q_block(x, up)
    forward_x(vo)
    w_got(uo, c)
    w_got(uo, d)
    q_block(x, uo)
    send_q(0, x)
    kv_block(x)
    send_kv(0, x)

    def near_group(g, xx, k):
        for vv in (v, vm, vp, vo):
            wide_got(xx, vv, k)
        for vv, kk in ((vm, d), (vp, c), (vo, c), (vo, d)):
            thin_got(xx, vv, kk)

        @pl.loop(0, 4)
        def _(uu):
            q_block(xx, uu)

        send_q(g, xx)
        kv_block(xx)
        send_kv(g, xx)

    near_group(1, xm, d)
    add_kv(0, x)
    add_q(x)
    near_group(2, xp, c)
    add_kv(1, xm)
    add_q(xm)
    share_kv(0)

    for vv, kk in ((vm, d), (vp, c), (vo, c), (vo, d)):
        thin_got(xo, vv, kk)

    def far_rows(t, vv):
        @pl.loop(0, 4)
        def _(uu):
            right = jnp.concatenate([wq[uu, 0], wq[uu, 1]], axis=1)
            value = jnp.dot(rows[xo, vv].reshape(64, half), right, preferred_element_type=jnp.float32)
            for k in (0, 1):
                q_part[xo, uu, k, vv] = value[:, k * 128:(k + 1) * 128]

        for n, (uu, k) in enumerate(targets):
            send(q_part.at[xo, uu, k, vv], q_got.at[c, u, xo, vv], q_send_far.at[t, n], q_recv.at[c, u, xo], chip(x, uu, v) + k)
        q_got[c, u, xo, vv] = q_part[xo, u, c, vv]

    for t, vv in enumerate((v, vm, vp, vo)):
        wide_got(xo, vv, c)
        wide_got(xo, vv, d)
        if t == 3:
            kv_block(xo)
            send_kv(3, xo)
        far_rows(t, vv)
        if t == 0:
            add_kv(2, xp)
            add_q(xp)
            share_kv(1)
        if t == 1:
            share_kv(2)
    add_kv(3, xo)
    add_q(xo)
    share_kv(3)
    finish_kv()

    got(other, row_send.at[0])
    for n, kind in enumerate(counts["kinds"]):
        got(rows.at[0, 0, 0, :, kind], row_send.at[n + 1])
    for n in range(counts["w"]):
        got(wq.at[0, 0], w_send.at[n, 0])
        got(wkv.at[0, 0], w_send.at[n, 1])
    for n in range(len(targets)):
        for g in range(3):
            got(q_part.at[0, 0, 0], q_send.at[g, n])
        for t in range(4):
            got(q_part.at[0, 0, 0, 0], q_send_far.at[t, n])
            got(kv_part.at[0, 0, 0], kv_send.at[t, n])
    for g in range(4):
        for n in range(1, 8):
            got(pieces.at[0, 0, 0], piece_send.at[g, n])
        got(pieces.at[0, 0], pair_send.at[g])


def solution(mesh):
    def local_step(x_rows, norm_gain, w_q, w_k, w_v):
        depth = x_rows.shape[1]
        half = depth // 2
        any_space = pl.BlockSpec(memory_space=pl.ANY)
        vmem = pl.BlockSpec(memory_space=pltpu.VMEM)
        bf16, f32 = jnp.bfloat16, jnp.float32
        out = jax.ShapeDtypeStruct((4, 4, 4, 64, 128), bf16)
        outs = pl.pallas_call(
            functools.partial(kernel, depth, half - half // 8),
            out_shape=(out, out, out),
            in_specs=[any_space, vmem, any_space, any_space, any_space],
            out_specs=(vmem, vmem, vmem),
            scratch_shapes=[
                pltpu.VMEM((32, depth), bf16),
                pltpu.VMEM((32, half), bf16),
                pltpu.VMEM((16, half), bf16),
                pltpu.VMEM((4, 4, 2, 32, half), bf16),
                pltpu.VMEM((4, 2, half, 128), bf16),
                pltpu.VMEM((4, 2, 16, half), bf16),
                pltpu.VMEM((4, 4, 2, 4, 64, 128), f32),
                pltpu.VMEM((4, 4, 2, 16, 256), f32),
                pltpu.VMEM((2, 4, 4, 4, 64, 128), f32),
                pltpu.VMEM((2, 4, 4, 16, 256), f32),
                pltpu.VMEM((2, 4, 8, 16, 1024), bf16),
                DMA((6,)),
                DMA((4, 4, 2)),
                DMA((4, 4, 2)),
                DMA((61,)),
                DMA((4, 2)),
                DMA((4, 2)),
                DMA((7, 2)),
                DMA((3, 7)),
                DMA((4, 7)),
                DMA((4, 7)),
                DMA((2, 4, 4)),
                DMA((2, 4, 4)),
                DMA((4, 8)),
                DMA((4, 8)),
                DMA((4,)),
                DMA((4,)),
            ],
            compiler_params=pltpu.CompilerParams(collective_id=0, has_side_effects=True, vmem_limit_bytes=67043328),
        )(x_rows, norm_gain.reshape(1, depth), w_q.reshape(depth, 128), w_k.T, w_v.T)
        return tuple(value.reshape(4096, 1, 128) for value in outs)

    return jax.shard_map(
        local_step,
        mesh=mesh,
        in_specs=(P(("dp", "tp"), None), P(None), P(None, "tp", None), P(None, "tp"), P(None, "tp")),
        out_specs=(P("dp", "tp", None), P("dp", "tp", None), P("dp", "tp", None)),
        check_vma=False,
    )
```

time: 505 us -> 177 us (0.35)
  waiting for transfers between devices: 296 us -> 0 us
  Pallas kernels: 0 us -> 170 us
  matrix products: 144 us -> 0 us
  starting transfers between devices: 41.1 us -> 0 us
  between operations: 14.3 us -> 0.65 us
  other arithmetic: 6.51 us -> 0 us
    all_gather x1 -> x0, waiting for transfers between devices: 287 us -> none  [local_step(): gathered = lax.all_gather(normed, 'tp', axis=0, tiled=True)]
    pallas_call x0 -> x1, Pallas kernels: none -> 170 us  [local_step(): pl.pallas_call(functools.partial(kernel, depth, half - half // 8), out_sh...]
    dot_general x3 -> x0, matrix products: 144 us -> none  [the longest x1 48.8 us: local_step(): jnp.einsum('td,dhe->the', gathered, w_q, preferred_element_type=jnp.float32)]
    ppermute x30 -> x0, starting transfers between devices: 41.1 us -> none  [head_pieces(): received.append(lax.ppermute(piece, 'tp', send_pairs))]
    ppermute x30 -> x0, waiting for transfers between devices: 9.32 us -> none  [head_pieces(): received.append(lax.ppermute(piece, 'tp', send_pairs))]
    unnamed x34 -> x5, local copies, waits for them, and re-layouts: 0.17 us -> 5.59 us
  transfers between devices with their start and end apart: 31 -> 0, of which waited for: 7 -> 0; matrix products, arithmetic and copies ran while one was open for 19% -> 0% of each run, Pallas kernels for 0% -> 0%
where the time goes in v2:
time: 177 us; the launch traced here: 176 us
  Pallas kernels  170 us (96%)
  local copies, waits for them, and re-layouts  5.59 us (3%)
    pallas_call x1, Pallas kernels, local_step(): pl.pallas_call(functools.partial(kernel, depth, half - half // 8), out_sh...  170 us
    unnamed x5, local copies, waits for them, and re-layouts  5.59 us

profile of v2, /device:TPU:1, one launch (start us, length us, event | category | flops | bytes accessed | tf_op | source)
XLA Modules:
  0.0 176.3 jit_solution(9067582394142007568)
XLA Ops:
  0.6 170.1 %shard_map.76 = (bf16[4,4,4,64,128]{4,3,2,1,0:T(8,128)(2,1)}, bf16[4,4,4,64,128]{4,3,2,1,0:T(8,128)(2,1)}, bf16[4,4,4,64,128]{4,3,2,1,0:T(8,128)(2,1)}) custom-call(bf16[32,16384]{1,0:T(8,128)(2,1)} %x_hbm.1, f32[1,16384]{1,0:T(1,128)} %bitcast.13, bf16[16384,128]{1,0:T(8,128)(2,1)} %bitcast.7, bf16[8,16384]{1,0:T(8,128)(2,1)} %bitcast.11, ...), custom_call_target="tpu_custom_call" | custom-call | tf_op jit(solution)/shard_map/pallas_call | solution.py:380
  170.7 0.0 copy-start
  170.7 2.4 %copy.11 = bf16[4096,1,128]{2,0,1:T(8,128)(2,1)} copy(bf16[4096,1,128]{2,0,1:T(8,128)(2,1)} %bitcast.10) | data formatting | bytes 2097152
  173.1 2.3 %copy.12 = bf16[4096,1,128]{2,0,1:T(8,128)(2,1)} copy(bf16[4096,1,128]{2,0,1:T(8,128)(2,1)} %bitcast.9) | data formatting | bytes 2097152
  175.4 0.0 copy-done
  175.4 1.0 copy.13
Async XLA Ops:
  170.7 4.6 %copy-start = (bf16[4,4,4,64,128]{4,3,2,1,0:T(8,128)(2,1)S(1)}, bf16[4,4,4,64,128]{4,3,2,1,0:T(8,128)(2,1)}, u32[]{:S(2)}) copy-start(bf16[4,4,4,64,128]{4,3,2,1,0:T(8,128)(2,1)} %get-tuple-element.8) | copy-start | bytes 3145732

commit v3 on v2

--- a/solution.py
+++ b/solution.py
@@ -19,7 +19,8 @@
 def kernel(
     depth, split, x_hbm, gain, wq_hbm, wk_hbm, wv_hbm, q_out, k_out, v_out,
     x_in, other, wkv_other, rows, wq, wkv, q_part, kv_part, q_got, kv_got, pieces,
-    load_sem, wide_recv, thin_recv, row_send, wq_recv, wkv_recv, w_send, q_send, q_send_far, kv_send, q_recv, kv_recv,
+    load_sem, wide_recv, thin_recv, row_send, wq_recv, wkv_recv, wq_send, wkv_send, q_send, q_send_far, kv_send, q_recv,
+    kv_recv,
     piece_send, piece_recv, pair_send, pair_recv,
 ):
     half = depth // 2
@@ -101,7 +102,7 @@
         load.wait()
     pl.semaphore_wait(barrier, len(peers))
 
-    counts = {"row": 0, "w": 0, "kinds": []}
+    counts = {"row": 0, "wq": 0, "wkv": 0, "kinds": []}
     wide, thin = slice(0, split), slice(split, half)
 
     def row_sem():
@@ -124,16 +125,18 @@
     def thin_got(xx, vv, k):
         got(rows.at[xx, vv, k, :, thin], thin_recv.at[xx, vv, k])
 
-    def send_w(q_src, kv_src, uu, k, target):
-        send(q_src, wq.at[uu, k], w_send.at[counts["w"], 0], wq_recv.at[uu, k], target)
-        send(kv_src, wkv.at[uu, k], w_send.at[counts["w"], 1], wkv_recv.at[uu, k], target)
-        counts["w"] += 1
-
-    def pass_w(uu, k, target):
-        send_w(wq.at[uu, k], wkv.at[uu, k], uu, k, target)
-
-    def w_got(uu, k):
+    def send_wq(src, uu, k, target):
+        send(src, wq.at[uu, k], wq_send.at[counts["wq"]], wq_recv.at[uu, k], target)
+        counts["wq"] += 1
+
+    def send_wkv(src, uu, k, target):
+        send(src, wkv.at[uu, k], wkv_send.at[counts["wkv"]], wkv_recv.at[uu, k], target)
+        counts["wkv"] += 1
+
+    def wq_got(uu, k):
         got(wq.at[uu, k], wq_recv.at[uu, k])
+
+    def wkv_got(uu, k):
         got(wkv.at[uu, k], wkv_recv.at[uu, k])
 
     x_next, x_last = chip(plus(x, 1), u, v) + c, chip(plus(x, 3), u, v) + c
@@ -143,69 +146,48 @@
     vp, vm, vo = plus(v, 1), plus(v, 3), plus(v, 2)
     up, um, uo = plus(u, 1), plus(u, 3), plus(u, 2)
 
+    near_x, near_v, near_u = (x_next, x_last), (v_next, v_last), (u_next, u_last)
+    x_far, v_far, u_far = chip(xo, u, v) + c, chip(x, u, vo) + c, chip(x, uo, v) + c
+
     send(other, rows.at[x, u, c], row_sem(), wide_recv.at[x, u, c], mate)
-    send_thin(x, v, c, x_next, x_last)
-    send_wide(x, v, c, v_next, v_last)
-    send_w(wq_hbm.at[own_columns, :], wkv.at[u, c], u, c, u_next)
-    send_w(wq_hbm.at[own_columns, :], wkv.at[u, c], u, c, u_last)
-    send_w(wq_hbm.at[mate_columns, :], wkv_other, v, c, mate)
+    send_thin(x, v, c, *near_x, x_far)
+    send_wide(x, v, c, *near_v, v_far)
+    for target in (*near_u, u_far):
+        send_wkv(wkv.at[u, c], u, c, target)
+    for target in near_u:
+        send_wq(wq_hbm.at[own_columns, :], u, c, target)
+    send_wkv(wkv_other, v, c, mate)
+    send_wq(wq_hbm.at[mate_columns, :], v, c, mate)
     got(rows.at[x, v, d], wide_recv.at[x, v, d])
-    send_thin(x, v, d, x_next, x_last)
-    send_wide(x, v, c, x_next, x_last)
-    send_wide(x, v, d, x_next, x_last, v_next, v_last)
+    send_thin(x, v, d, *near_x, x_far)
+    send_wide(x, v, c, *near_x)
+    send_wide(x, v, d, *near_v, v_far)
+    send_wide(x, v, d, *near_x)
     for k in (c, d):
-        send_thin(x, v, k, v_next, v_last)
-    w_got(u, d)
-    pass_w(u, d, u_next)
-    pass_w(u, d, u_last)
-
-    thin_got(xm, v, c)
-    send_thin(xm, v, c, x_next)
-    thin_got(xp, v, d)
-    send_thin(xp, v, d, x_last)
-    thin_got(xm, v, d)
-    thin_got(xp, v, c)
-    for xx in (xm, xp):
-        for k in (c, d):
-            send_thin(xx, v, k, v_next, v_last)
-
-    wide_got(x, vm, c)
-    send_wide(x, vm, c, v_next)
-    wide_got(xm, v, c)
-    send_wide(xm, v, c, x_next)
-    wide_got(x, vp, c)
-    for vv in (vm, vp):
-        send_wide(x, vv, c, x_next, x_last)
-    wide_got(x, vp, d)
-    send_wide(x, vp, d, v_last)
-    wide_got(xp, v, d)
-    send_wide(xp, v, d, x_last)
-    wide_got(x, vm, d)
-    for vv in (vm, vp):
-        send_wide(x, vv, d, x_next, x_last)
+        send_thin(x, v, k, *near_v, v_far)
+    wkv_got(u, d)
+    for target in (*near_u, u_far):
+        send_wkv(wkv.at[u, d], u, d, target)
+    wq_got(u, d)
+    for target in near_u:
+        send_wq(wq.at[u, d], u, d, target)
+    send_wq(wq_hbm.at[own_columns, :], u, c, u_far)
+    send_wq(wq.at[u, d], u, d, u_far)
+
+    for xx in (xm, xp, xo):
+        for k in (c, d):
+            thin_got(xx, v, k)
+            send_thin(xx, v, k, *near_v, v_far)
     for k in (c, d):
-        thin_got(xo, v, k)
-        send_thin(xo, v, k, v_next, v_last)
+        for vv in (vm, vp):
+            wide_got(x, vv, k)
+            send_wide(x, vv, k, *near_x)
     for k in (c, d):
         wide_got(x, vo, k)
-        send_wide(x, vo, k, x_next, x_last)
-    for xx in (x, xm, xp, xo):
-        thin_got(xx, vm, c)
-        send_thin(xx, vm, c, v_next)
-        thin_got(xx, vp, d)
-        send_thin(xx, vp, d, v_last)
-
-    def forward_x(vv):
-        wide_got(xm, vv, c)
-        send_wide(xm, vv, c, x_next)
-        wide_got(xp, vv, d)
-        send_wide(xp, vv, d, x_last)
-
-    targets = []
-    for du in range(4):
-        for dk in (0, 1):
-            if du or dk:
-                targets.append((plus(u, du), rem(c + dk, 2)))
+        send_wide(x, vo, k, *near_x)
+    for vv in (v, vp, vm, vo):
+        for k in (c, d):
+            send_wide(x, vv, k, x_far)
 
     def q_block(xx, uu):
         right = jnp.concatenate([wq[uu, 0], wq[uu, 1]], axis=1)
@@ -213,21 +195,52 @@
         for k in (0, 1):
             q_part[xx, uu, k] = value[:, k * 128:(k + 1) * 128].reshape(4, 64, 128)
 
-    def kv_block(xx):
+    def send_q(g, xx, du):
+        uu = plus(u, du)
+        for k in ((c, d) if du else (d,)):
+            send(q_part.at[xx, uu, k], q_got.at[c, u, xx], q_send.at[g, du, k], q_recv.at[c, u, xx], chip(x, uu, v) + k)
+
+    def kv_group(g, xx):
         value = lax.dot_general(
             wkv[...].reshape(128, half), rows[xx].reshape(256, half), (((1,), (1,)), ((), ())), preferred_element_type=jnp.float32
         )
         kv_part[xx] = value.reshape(4, 2, 16, 256)
-
-    def send_q(g, xx):
-        for n, (uu, k) in enumerate(targets):
-            send(q_part.at[xx, uu, k], q_got.at[c, u, xx], q_send.at[g, n], q_recv.at[c, u, xx], chip(x, uu, v) + k)
-        q_got[c, u, xx] = q_part[xx, u, c]
-
-    def send_kv(g, xx):
-        for n, (uu, k) in enumerate(targets):
-            send(kv_part.at[xx, uu, k], kv_got.at[c, u, xx], kv_send.at[g, n], kv_recv.at[c, u, xx], chip(x, uu, v) + k)
+        for du in (2, 1, 3, 0):
+            uu = plus(u, du)
+            for k in ((c, d) if du else (d,)):
+                send(kv_part.at[xx, uu, k], kv_got.at[c, u, xx], kv_send.at[g, du, k], kv_recv.at[c, u, xx], chip(x, uu, v) + k)
         kv_got[c, u, xx] = kv_part[xx, u, c]
+
+    def far_rows(t):
+        vv = plus(v, t + t // 2 - 2 * (t // 3))
+        wide_got(xo, vv, c)
+        wide_got(xo, vv, d)
+
+        @pl.when(t == 3)
+        def _():
+            kv_group(3, xo)
+
+        @pl.loop(0, 4)
+        def _(j):
+            uu = plus(u, 2 + j)
+            right = jnp.concatenate([wq[uu, 0], wq[uu, 1]], axis=1)
+            value = jnp.dot(rows[xo, vv].reshape(64, half), right, preferred_element_type=jnp.float32)
+            for k in (0, 1):
+                q_part[xo, uu, k, vv] = value[:, k * 128:(k + 1) * 128]
+
+            def send_far(k):
+                send(
+                    q_part.at[xo, uu, k, vv], q_got.at[c, u, xo, vv], q_send_far.at[t, uu, k], q_recv.at[c, u, xo],
+                    chip(x, uu, v) + k,
+                )
+
+            send_far(d)
+
+            @pl.when(j != 2)
+            def _():
+                send_far(c)
+
+        q_got[c, u, xo, vv] = q_part[xo, u, c, vv]
 
     senders = [(c, plus(u, n)) for n in (1, 2, 3)] + [(d, n) for n in range(4)]
     place = rem(y, 2) * 4 + x
@@ -266,87 +279,84 @@
         def _(zz):
             columns = pl.ds(pl.multiple_of(zz * 256, 256), 256)
             for xx in range(4):
-                places = [((0, 2, 3, 1)[(xx - n) % 4], n) for n in range(8)]
+                places = [((xx - n + 1) % 4, n) for n in range(8)]
                 wide_pieces = [pieces[k, g, n, :, columns].astype(jnp.float32) for g, n in places for k in (0, 1)]
                 for out, first in ((k_out, 0), (v_out, 8)):
                     value = jnp.concatenate([w[first:first + 8] for w in wide_pieces], axis=0).T.astype(jnp.bfloat16)
                     out[zz, :, xx] = value.reshape(4, 64, 128)
 
-    w_got(um, c)
-    pass_w(um, c, u_next)
-    forward_x(vm)
     load_wq.wait()
+    for vv in (vm, vp, vo):
+        for k in (c, d):
+            thin_got(x, vv, k)
+
+    @pl.loop(0, 1)
+    def _(i):
+        q_block(x, plus(u, i))
+
+    for uu in (um, up, uo):
+        for k in (c, d):
+            wkv_got(uu, k)
+    for uu in (um, up):
+        for k in (c, d):
+            wq_got(uu, k)
+
+    @pl.loop(0, 2)
+    def _(i):
+        q_block(x, plus(um, 2 * i))
+
+    for xx in (xm, xp):
+        for k in (c, d):
+            wide_got(xx, v, k)
+            for vv in (vm, vp, vo):
+                wide_got(xx, vv, k)
+                thin_got(xx, vv, k)
+
+    @pl.loop(0, 3)
+    def _(g):
+        kv_group(g, plus(xm, g))
+
+    @pl.loop(0, 2)
+    def _(i):
+        @pl.loop(0, 3)
+        def _(j):
+            q_block(plus(xm, 2 * i), plus(um, j))
+
     for k in (c, d):
-        thin_got(x, vo, k)
-    for vv, k in ((vm, d), (vp, c)):
-        thin_got(x, vv, k)
-    q_block(x, u)
-    w_got(up, d)
-    pass_w(up, d, u_last)
-    forward_x(vp)
-    w_got(um, d)
-    w_got(up, c)
-    q_block(x, um)
-    q_block(x, up)
-    forward_x(vo)
-    w_got(uo, c)
-    w_got(uo, d)
-    q_block(x, uo)
-    send_q(0, x)
-    kv_block(x)
-    send_kv(0, x)
-
-    def near_group(g, xx, k):
-        for vv in (v, vm, vp, vo):
-            wide_got(xx, vv, k)
-        for vv, kk in ((vm, d), (vp, c), (vo, c), (vo, d)):
-            thin_got(xx, vv, kk)
-
-        @pl.loop(0, 4)
-        def _(uu):
-            q_block(xx, uu)
-
-        send_q(g, xx)
-        kv_block(xx)
-        send_kv(g, xx)
-
-    near_group(1, xm, d)
-    add_kv(0, x)
-    add_q(x)
-    near_group(2, xp, c)
-    add_kv(1, xm)
-    add_q(xm)
-    share_kv(0)
-
-    for vv, kk in ((vm, d), (vp, c), (vo, c), (vo, d)):
-        thin_got(xo, vv, kk)
-
-    def far_rows(t, vv):
-        @pl.loop(0, 4)
-        def _(uu):
-            right = jnp.concatenate([wq[uu, 0], wq[uu, 1]], axis=1)
-            value = jnp.dot(rows[xo, vv].reshape(64, half), right, preferred_element_type=jnp.float32)
-            for k in (0, 1):
-                q_part[xo, uu, k, vv] = value[:, k * 128:(k + 1) * 128]
-
-        for n, (uu, k) in enumerate(targets):
-            send(q_part.at[xo, uu, k, vv], q_got.at[c, u, xo, vv], q_send_far.at[t, n], q_recv.at[c, u, xo], chip(x, uu, v) + k)
-        q_got[c, u, xo, vv] = q_part[xo, u, c, vv]
-
-    for t, vv in enumerate((v, vm, vp, vo)):
-        wide_got(xo, vv, c)
-        wide_got(xo, vv, d)
-        if t == 3:
-            kv_block(xo)
-            send_kv(3, xo)
-        far_rows(t, vv)
-        if t == 0:
-            add_kv(2, xp)
-            add_q(xp)
-            share_kv(1)
-        if t == 1:
-            share_kv(2)
+        wq_got(uo, k)
+
+    @pl.loop(0, 3)
+    def _(g):
+        for du in (1, 3, 0):
+            send_q(g, plus(xm, g), du)
+
+    @pl.loop(0, 3)
+    def _(g):
+        xx = plus(xm, g)
+        q_block(xx, uo)
+        send_q(g, xx, 2)
+        q_got[c, u, xx] = q_part[xx, u, c]
+
+    for vv in (vm, vp, vo):
+        for k in (c, d):
+            thin_got(xo, vv, k)
+
+    @pl.loop(0, 3)
+    def _(t):
+        far_rows(t)
+
+    for g in range(3):
+        add_kv(g, plus(xm, g))
+
+    @pl.loop(3, 4)
+    def _(t):
+        far_rows(t)
+
     add_kv(3, xo)
+    for g in range(3):
+        add_q(plus(xm, g))
+    for g in range(3):
+        share_kv(g)
     add_q(xo)
     share_kv(3)
     finish_kv()
@@ -354,15 +364,17 @@
     got(other, row_send.at[0])
     for n, kind in enumerate(counts["kinds"]):
         got(rows.at[0, 0, 0, :, kind], row_send.at[n + 1])
-    for n in range(counts["w"]):
-        got(wq.at[0, 0], w_send.at[n, 0])
-        got(wkv.at[0, 0], w_send.at[n, 1])
-    for n in range(len(targets)):
-        for g in range(3):
-            got(q_part.at[0, 0, 0], q_send.at[g, n])
-        for t in range(4):
-            got(q_part.at[0, 0, 0, 0], q_send_far.at[t, n])
-            got(kv_part.at[0, 0, 0], kv_send.at[t, n])
+    for n in range(counts["wq"]):
+        got(wq.at[0, 0], wq_send.at[n])
+    for n in range(counts["wkv"]):
+        got(wkv.at[0, 0], wkv_send.at[n])
+    for du in range(4):
+        for k in ((c, d) if du else (d,)):
+            for g in range(3):
+                got(q_part.at[0, 0, 0], q_send.at[g, du, k])
+            for t in range(4):
+                got(q_part.at[0, 0, 0, 0], q_send_far.at[t, plus(u, du), k])
+                got(kv_part.at[0, 0, 0], kv_send.at[t, du, k])
     for g in range(4):
         for n in range(1, 8):
             got(pieces.at[0, 0, 0], piece_send.at[g, n])
@@ -400,10 +412,11 @@
                 DMA((61,)),
                 DMA((4, 2)),
                 DMA((4, 2)),
-                DMA((7, 2)),
-                DMA((3, 7)),
-                DMA((4, 7)),
-                DMA((4, 7)),
+                DMA((7,)),
+                DMA((7,)),
+                DMA((3, 4, 2)),
+                DMA((4, 4, 2)),
+                DMA((4, 4, 2)),
                 DMA((2, 4, 4)),
                 DMA((2, 4, 4)),
                 DMA((4, 8)),

time: 177 us -> 199 us (1.12)
  Pallas kernels: 170 us -> 193 us
    pallas_call x1, Pallas kernels: 170 us -> 193 us  [local_step(): pl.pallas_call(functools.partial(kernel, depth, half - half // 8), out_sh...]
where the time goes in v3:
time: 199 us
  Pallas kernels  193 us (97%)
  local copies, waits for them, and re-layouts  5.59 us (3%)
    pallas_call x1, Pallas kernels, local_step(): pl.pallas_call(functools.partial(kernel, depth, half - half // 8), out_sh...  193 us
    unnamed x5, local copies, waits for them, and re-layouts  5.59 us

profile of v3, /device:TPU:1, one launch (start us, length us, event | category | flops | bytes accessed | tf_op | source)
XLA Modules:
  0.0 199.2 jit_solution(4040297880965231220)
XLA Ops:
  0.6 193.0 %shard_map.76 = (bf16[4,4,4,64,128]{4,3,2,1,0:T(8,128)(2,1)}, bf16[4,4,4,64,128]{4,3,2,1,0:T(8,128)(2,1)}, bf16[4,4,4,64,128]{4,3,2,1,0:T(8,128)(2,1)}) custom-call(bf16[32,16384]{1,0:T(8,128)(2,1)} %x_hbm.1, f32[1,16384]{1,0:T(1,128)} %bitcast.13, bf16[16384,128]{1,0:T(8,128)(2,1)} %bitcast.7, bf16[8,16384]{1,0:T(8,128)(2,1)} %bitcast.11, ...), custom_call_target="tpu_custom_call" | custom-call | tf_op jit(solution)/shard_map/pallas_call | solution.py:392
  193.6 0.0 copy-start
  193.6 2.4 %copy.11 = bf16[4096,1,128]{2,0,1:T(8,128)(2,1)} copy(bf16[4096,1,128]{2,0,1:T(8,128)(2,1)} %bitcast.10) | data formatting | bytes 2097152
  196.0 2.3 %copy.12 = bf16[4096,1,128]{2,0,1:T(8,128)(2,1)} copy(bf16[4096,1,128]{2,0,1:T(8,128)(2,1)} %bitcast.9) | data formatting | bytes 2097152
  198.2 0.0 copy-done
  198.2 1.0 copy.13
Async XLA Ops:
  193.6 4.6 %copy-start = (bf16[4,4,4,64,128]{4,3,2,1,0:T(8,128)(2,1)S(1)}, bf16[4,4,4,64,128]{4,3,2,1,0:T(8,128)(2,1)}, u32[]{:S(2)}) copy-start(bf16[4,4,4,64,128]{4,3,2,1,0:T(8,128)(2,1)} %get-tuple-element.8) | copy-start | bytes 3145732

commit v4 on v3

--- a/solution.py
+++ b/solution.py
@@ -147,47 +147,76 @@
     up, um, uo = plus(u, 1), plus(u, 3), plus(u, 2)
 
     near_x, near_v, near_u = (x_next, x_last), (v_next, v_last), (u_next, u_last)
-    x_far, v_far, u_far = chip(xo, u, v) + c, chip(x, u, vo) + c, chip(x, uo, v) + c
 
     send(other, rows.at[x, u, c], row_sem(), wide_recv.at[x, u, c], mate)
-    send_thin(x, v, c, *near_x, x_far)
-    send_wide(x, v, c, *near_v, v_far)
-    for target in (*near_u, u_far):
+    send_thin(x, v, c, *near_x)
+    send_wide(x, v, c, *near_v)
+    for target in near_u:
         send_wkv(wkv.at[u, c], u, c, target)
     for target in near_u:
         send_wq(wq_hbm.at[own_columns, :], u, c, target)
     send_wkv(wkv_other, v, c, mate)
     send_wq(wq_hbm.at[mate_columns, :], v, c, mate)
     got(rows.at[x, v, d], wide_recv.at[x, v, d])
-    send_thin(x, v, d, *near_x, x_far)
+    send_thin(x, v, d, *near_x)
     send_wide(x, v, c, *near_x)
-    send_wide(x, v, d, *near_v, v_far)
+    send_wide(x, v, d, *near_v)
     send_wide(x, v, d, *near_x)
     for k in (c, d):
-        send_thin(x, v, k, *near_v, v_far)
+        send_thin(x, v, k, *near_v)
     wkv_got(u, d)
-    for target in (*near_u, u_far):
+    for target in near_u:
         send_wkv(wkv.at[u, d], u, d, target)
     wq_got(u, d)
     for target in near_u:
         send_wq(wq.at[u, d], u, d, target)
-    send_wq(wq_hbm.at[own_columns, :], u, c, u_far)
-    send_wq(wq.at[u, d], u, d, u_far)
-
-    for xx in (xm, xp, xo):
+
+    def pass_thin_x(vv):
+        thin_got(xm, vv, c)
+        send_thin(xm, vv, c, x_next)
+        thin_got(xp, vv, d)
+        send_thin(xp, vv, d, x_last)
+
+    def pass_x(vv):
+        wide_got(xm, vv, c)
+        send_wide(xm, vv, c, x_next)
+        wide_got(xp, vv, d)
+        send_wide(xp, vv, d, x_last)
+
+    pass_thin_x(v)
+    thin_got(xm, v, d)
+    thin_got(xp, v, c)
+    for xx in (xm, xp):
         for k in (c, d):
-            thin_got(xx, v, k)
-            send_thin(xx, v, k, *near_v, v_far)
+            send_thin(xx, v, k, *near_v)
+
+    wide_got(x, vm, c)
+    send_wide(x, vm, c, v_next)
+    wkv_got(um, c)
+    send_wkv(wkv.at[um, c], um, c, u_next)
+    wide_got(xm, v, c)
+    send_wide(xm, v, c, x_next)
+    wide_got(x, vp, c)
+    for vv in (vm, vp):
+        send_wide(x, vv, c, *near_x)
+    wide_got(x, vp, d)
+    send_wide(x, vp, d, v_last)
+    wide_got(xp, v, d)
+    send_wide(xp, v, d, x_last)
+    wide_got(x, vm, d)
+    for vv in (vm, vp):
+        send_wide(x, vv, d, *near_x)
     for k in (c, d):
-        for vv in (vm, vp):
-            wide_got(x, vv, k)
-            send_wide(x, vv, k, *near_x)
+        thin_got(xo, v, k)
+        send_thin(xo, v, k, *near_v)
     for k in (c, d):
         wide_got(x, vo, k)
         send_wide(x, vo, k, *near_x)
-    for vv in (v, vp, vm, vo):
-        for k in (c, d):
-            send_wide(x, vv, k, x_far)
+    for xx in (x, xm, xp, xo):
+        thin_got(xx, vm, c)
+        send_thin(xx, vm, c, v_next)
+        thin_got(xx, vp, d)
+        send_thin(xx, vp, d, v_last)
 
     def q_block(xx, uu):
         right = jnp.concatenate([wq[uu, 0], wq[uu, 1]], axis=1)
@@ -212,7 +241,7 @@
         kv_got[c, u, xx] = kv_part[xx, u, c]
 
     def far_rows(t):
-        vv = plus(v, t + t // 2 - 2 * (t // 3))
+        vv = plus(v, t + 3)
         wide_got(xo, vv, c)
         wide_got(xo, vv, d)
 
@@ -286,31 +315,38 @@
                     out[zz, :, xx] = value.reshape(4, 64, 128)
 
     load_wq.wait()
-    for vv in (vm, vp, vo):
-        for k in (c, d):
-            thin_got(x, vv, k)
+    for vv, k in ((vm, d), (vp, c), (vo, c), (vo, d)):
+        thin_got(x, vv, k)
 
     @pl.loop(0, 1)
     def _(i):
         q_block(x, plus(u, i))
 
-    for uu in (um, up, uo):
-        for k in (c, d):
-            wkv_got(uu, k)
-    for uu in (um, up):
-        for k in (c, d):
-            wq_got(uu, k)
+    wq_got(um, c)
+    send_wq(wq.at[um, c], um, c, u_next)
+    wkv_got(up, d)
+    send_wkv(wkv.at[up, d], up, d, u_last)
+    pass_x(vm)
+    wq_got(up, d)
+    send_wq(wq.at[up, d], up, d, u_last)
+    pass_x(vp)
+    wq_got(um, d)
+    wq_got(up, c)
 
     @pl.loop(0, 2)
     def _(i):
         q_block(x, plus(um, 2 * i))
 
-    for xx in (xm, xp):
-        for k in (c, d):
-            wide_got(xx, v, k)
-            for vv in (vm, vp, vo):
-                wide_got(xx, vv, k)
-                thin_got(xx, vv, k)
+    pass_x(vo)
+    wkv_got(um, d)
+    wkv_got(up, c)
+    for k in (c, d):
+        wkv_got(uo, k)
+    for xx, k in ((xm, d), (xp, c)):
+        for vv in (v, vm, vp, vo):
+            wide_got(xx, vv, k)
+        for vv, kk in ((vm, d), (vp, c), (vo, c), (vo, d)):
+            thin_got(xx, vv, kk)
 
     @pl.loop(0, 3)
     def _(g):
@@ -337,9 +373,8 @@
         send_q(g, xx, 2)
         q_got[c, u, xx] = q_part[xx, u, c]
 
-    for vv in (vm, vp, vo):
-        for k in (c, d):
-            thin_got(xo, vv, k)
+    for vv, kk in ((vm, d), (vp, c), (vo, c), (vo, d)):
+        thin_got(xo, vv, kk)
 
     @pl.loop(0, 3)
     def _(t):

time: 199 us -> 167 us (0.84)
  Pallas kernels: 193 us -> 161 us
    pallas_call x1, Pallas kernels: 193 us -> 161 us  [local_step(): pl.pallas_call(functools.partial(kernel, depth, half - half // 8), out_sh...]
where the time goes in v4:
time: 167 us
  Pallas kernels  161 us (96%)
  local copies, waits for them, and re-layouts  5.59 us (3%)
    pallas_call x1, Pallas kernels, local_step(): pl.pallas_call(functools.partial(kernel, depth, half - half // 8), out_sh...  161 us
    unnamed x5, local copies, waits for them, and re-layouts  5.59 us

profile of v4, /device:TPU:1, one launch (start us, length us, event | category | flops | bytes accessed | tf_op | source)
XLA Modules:
  0.0 166.9 jit_solution(9943992478795395750)
XLA Ops:
  0.6 160.7 %shard_map.76 = (bf16[4,4,4,64,128]{4,3,2,1,0:T(8,128)(2,1)}, bf16[4,4,4,64,128]{4,3,2,1,0:T(8,128)(2,1)}, bf16[4,4,4,64,128]{4,3,2,1,0:T(8,128)(2,1)}) custom-call(bf16[32,16384]{1,0:T(8,128)(2,1)} %x_hbm.1, f32[1,16384]{1,0:T(1,128)} %bitcast.13, bf16[16384,128]{1,0:T(8,128)(2,1)} %bitcast.7, bf16[8,16384]{1,0:T(8,128)(2,1)} %bitcast.11, ...), custom_call_target="tpu_custom_call" | custom-call | tf_op jit(solution)/shard_map/pallas_call | solution.py:427
  161.3 0.0 copy-start
  161.3 2.4 %copy.11 = bf16[4096,1,128]{2,0,1:T(8,128)(2,1)} copy(bf16[4096,1,128]{2,0,1:T(8,128)(2,1)} %bitcast.10) | data formatting | bytes 2097152
  163.7 2.3 %copy.12 = bf16[4096,1,128]{2,0,1:T(8,128)(2,1)} copy(bf16[4096,1,128]{2,0,1:T(8,128)(2,1)} %bitcast.9) | data formatting | bytes 2097152
  165.9 0.0 copy-done
  165.9 1.0 copy.13
Async XLA Ops:
  161.3 4.6 %copy-start = (bf16[4,4,4,64,128]{4,3,2,1,0:T(8,128)(2,1)S(1)}, bf16[4,4,4,64,128]{4,3,2,1,0:T(8,128)(2,1)}, u32[]{:S(2)}) copy-start(bf16[4,4,4,64,128]{4,3,2,1,0:T(8,128)(2,1)} %get-tuple-element.8) | copy-start | bytes 3145732

commit v5 on v4

--- a/solution.py
+++ b/solution.py
@@ -224,10 +224,17 @@
         for k in (0, 1):
             q_part[xx, uu, k] = value[:, k * 128:(k + 1) * 128].reshape(4, 64, 128)
 
-    def send_q(g, xx, du):
+    def send_q(g, xx, du, whole=True):
         uu = plus(u, du)
-        for k in ((c, d) if du else (d,)):
+
+        def to(k):
             send(q_part.at[xx, uu, k], q_got.at[c, u, xx], q_send.at[g, du, k], q_recv.at[c, u, xx], chip(x, uu, v) + k)
+
+        to(d)
+
+        @pl.when(whole)
+        def _():
+            to(c)
 
     def kv_group(g, xx):
         value = lax.dot_general(
@@ -274,16 +281,29 @@
     senders = [(c, plus(u, n)) for n in (1, 2, 3)] + [(d, n) for n in range(4)]
     place = rem(y, 2) * 4 + x
 
-    def add_kv(g, xx):
+    def add_kv(g, xx, direct=False):
         for role, n in senders:
             got(kv_got.at[role, n, xx], kv_recv.at[role, n, xx])
         for zz in range(4):
             second = jnp.concatenate([kv_got[1, yy, xx][:, zz * 64:(zz + 1) * 64] for yy in range(4)], axis=1)
             pieces[c, g, place, :, pl.ds(zz * 256, 256)] = (kv_got[0, zz, xx] + second).astype(jnp.bfloat16)
-        for n in range(1, 8):
-            there = rem(place + n, 8)
-            target = ((z * 4 + (y // 2) * 2 + there // 4) * 4 + rem(there, 4)) * 2 + c
-            send(pieces.at[c, g, place], pieces.at[c, g, place], piece_send.at[g, n], piece_recv.at[g, place], target)
+        own = pieces.at[c, g, place]
+        for n in range(1, 4):
+            send(own, own, piece_send.at[g, n], piece_recv.at[g, place], row_chip(n, y) + c)
+            if direct:
+                send(own, own, piece_send.at[g, n + 4], piece_recv.at[g, place], row_chip(n, y_pair) + c)
+        send(own, own, piece_send.at[g, 0], piece_recv.at[g, place], row_chip(0, y_pair) + c)
+
+    def row_chip(n, yy):
+        return ((z * 4 + yy) * 4 + plus(x, n)) * 2
+
+    pair_place = 4 - place + 2 * x
+
+    def pass_kv(g):
+        got(pieces.at[c, g, pair_place], piece_recv.at[g, pair_place])
+        theirs = pieces.at[c, g, pair_place]
+        for n in range(1, 4):
+            send(theirs, theirs, piece_send.at[g, n + 4], piece_recv.at[g, pair_place], row_chip(n, y) + c)
 
     def add_q(xx):
         for role, n in senders:
@@ -294,9 +314,9 @@
             for yy in range(4):
                 q_out[zz, yy, xx] = (q_got[0, zz, xx, yy] + q_got[1, yy, xx, zz]).astype(jnp.bfloat16)
 
-    def share_kv(g):
-        for n in range(1, 8):
-            there = rem(place + n, 8)
+    def share_kv(g, passed=True):
+        for n in (1, 2, 3, 5, 6, 7) if passed else range(1, 8):
+            there = (pair_place if n >= 4 else place) - x + plus(x, n)
             got(pieces.at[c, g, there], piece_recv.at[g, there])
         send(pieces.at[c, g], pieces.at[c, g], pair_send.at[g], pair_recv.at[g], mate)
 
@@ -321,6 +341,7 @@
     @pl.loop(0, 1)
     def _(i):
         q_block(x, plus(u, i))
+        send_q(1, x, 0, False)
 
     wq_got(um, c)
     send_wq(wq.at[um, c], um, c, u_next)
@@ -336,6 +357,7 @@
     @pl.loop(0, 2)
     def _(i):
         q_block(x, plus(um, 2 * i))
+        send_q(1, x, plus(2 * i, 3))
 
     pass_x(vo)
     wkv_got(um, d)
@@ -357,14 +379,10 @@
         @pl.loop(0, 3)
         def _(j):
             q_block(plus(xm, 2 * i), plus(um, j))
+            send_q(2 * i, plus(xm, 2 * i), plus(j, 3), j != 1)
 
     for k in (c, d):
         wq_got(uo, k)
-
-    @pl.loop(0, 3)
-    def _(g):
-        for du in (1, 3, 0):
-            send_q(g, plus(xm, g), du)
 
     @pl.loop(0, 3)
     def _(g):
@@ -387,14 +405,10 @@
     def _(t):
         far_rows(t)
 
-    add_kv(3, xo)
+    for g in range(3):
+        pass_kv(g)
     for g in range(3):
         add_q(plus(xm, g))
-    for g in range(3):
-        share_kv(g)
-    add_q(xo)
-    share_kv(3)
-    finish_kv()
 
     got(other, row_send.at[0])
     for n, kind in enumerate(counts["kinds"]):
@@ -403,15 +417,30 @@
         got(wq.at[0, 0], wq_send.at[n])
     for n in range(counts["wkv"]):
         got(wkv.at[0, 0], wkv_send.at[n])
-    for du in range(4):
-        for k in ((c, d) if du else (d,)):
+
+    @pl.loop(0, 4)
+    def _(du):
+        def drained(k):
             for g in range(3):
                 got(q_part.at[0, 0, 0], q_send.at[g, du, k])
             for t in range(4):
                 got(q_part.at[0, 0, 0, 0], q_send_far.at[t, plus(u, du), k])
                 got(kv_part.at[0, 0, 0], kv_send.at[t, du, k])
+
+        drained(d)
+
+        @pl.when(du > 0)
+        def _():
+            drained(c)
+
+    add_kv(3, xo, direct=True)
+    for g in range(3):
+        share_kv(g)
+    add_q(xo)
+    share_kv(3, passed=False)
+    finish_kv()
     for g in range(4):
-        for n in range(1, 8):
+        for n in (0, 1, 2, 3, 5, 6, 7):
             got(pieces.at[0, 0, 0], piece_send.at[g, n])
         got(pieces.at[0, 0], pair_send.at[g])
 

time: 167 us -> 161 us (0.964)
  Pallas kernels: 161 us -> 155 us
    pallas_call x1, Pallas kernels: 161 us -> 155 us  [local_step(): pl.pallas_call(functools.partial(kernel, depth, half - half // 8), out_sh...]
where the time goes in v5:
time: 161 us
  Pallas kernels  155 us (96%)
  local copies, waits for them, and re-layouts  5.59 us (3%)
    pallas_call x1, Pallas kernels, local_step(): pl.pallas_call(functools.partial(kernel, depth, half - half // 8), out_sh...  155 us
    unnamed x5, local copies, waits for them, and re-layouts  5.59 us

profile of v5, /device:TPU:1, one launch (start us, length us, event | category | flops | bytes accessed | tf_op | source)
XLA Modules:
  0.0 161.0 jit_solution(14468227007549600507)
XLA Ops:
  0.6 154.8 %shard_map.76 = (bf16[4,4,4,64,128]{4,3,2,1,0:T(8,128)(2,1)}, bf16[4,4,4,64,128]{4,3,2,1,0:T(8,128)(2,1)}, bf16[4,4,4,64,128]{4,3,2,1,0:T(8,128)(2,1)}) custom-call(bf16[32,16384]{1,0:T(8,128)(2,1)} %x_hbm.1, f32[1,16384]{1,0:T(1,128)} %bitcast.13, bf16[16384,128]{1,0:T(8,128)(2,1)} %bitcast.7, bf16[8,16384]{1,0:T(8,128)(2,1)} %bitcast.11, ...), custom_call_target="tpu_custom_call" | custom-call | tf_op jit(solution)/shard_map/pallas_call | solution.py:456
  155.4 0.0 copy-start
  155.4 2.4 %copy.11 = bf16[4096,1,128]{2,0,1:T(8,128)(2,1)} copy(bf16[4096,1,128]{2,0,1:T(8,128)(2,1)} %bitcast.10) | data formatting | bytes 2097152
  157.8 2.3 %copy.12 = bf16[4096,1,128]{2,0,1:T(8,128)(2,1)} copy(bf16[4096,1,128]{2,0,1:T(8,128)(2,1)} %bitcast.9) | data formatting | bytes 2097152
  160.0 0.0 copy-done
  160.0 1.0 copy.13
Async XLA Ops:
  155.4 4.6 %copy-start = (bf16[4,4,4,64,128]{4,3,2,1,0:T(8,128)(2,1)S(1)}, bf16[4,4,4,64,128]{4,3,2,1,0:T(8,128)(2,1)}, u32[]{:S(2)}) copy-start(bf16[4,4,4,64,128]{4,3,2,1,0:T(8,128)(2,1)} %get-tuple-element.8) | copy-start | bytes 3145732

commit v6 on v5

--- a/solution.py
+++ b/solution.py
@@ -17,11 +17,11 @@
 
 
 def kernel(
-    depth, split, x_hbm, gain, wq_hbm, wk_hbm, wv_hbm, q_out, k_out, v_out,
-    x_in, other, wkv_other, rows, wq, wkv, q_part, kv_part, q_got, kv_got, pieces,
+    depth, split, x_hbm, gain, wq_hbm, wk_hbm, wv_hbm, q_hbm, pieces_hbm,
+    x_in, other, wkv_other, rows, wq, wkv, q_part, kv_part, q_got, kv_got, q_sum, pieces,
     load_sem, wide_recv, thin_recv, row_send, wq_recv, wkv_recv, wq_send, wkv_send, q_send, q_send_far, kv_send, q_recv,
     kv_recv,
-    piece_send, piece_recv, pair_send, pair_recv,
+    piece_send, piece_recv, pair_send, pair_recv, q_left, pieces_left,
 ):
     half = depth // 2
     me = lax.axis_index("tp")
@@ -247,16 +247,8 @@
                 send(kv_part.at[xx, uu, k], kv_got.at[c, u, xx], kv_send.at[g, du, k], kv_recv.at[c, u, xx], chip(x, uu, v) + k)
         kv_got[c, u, xx] = kv_part[xx, u, c]
 
-    def far_rows(t):
-        vv = plus(v, t + 3)
-        wide_got(xo, vv, c)
-        wide_got(xo, vv, d)
-
-        @pl.when(t == 3)
-        def _():
-            kv_group(3, xo)
-
-        @pl.loop(0, 4)
+    def far_rows(t, vv, first, last):
+        @pl.loop(first, last)
         def _(j):
             uu = plus(u, 2 + j)
             right = jnp.concatenate([wq[uu, 0], wq[uu, 1]], axis=1)
@@ -264,19 +256,21 @@
             for k in (0, 1):
                 q_part[xo, uu, k, vv] = value[:, k * 128:(k + 1) * 128]
 
-            def send_far(k):
+            def to(k):
                 send(
                     q_part.at[xo, uu, k, vv], q_got.at[c, u, xo, vv], q_send_far.at[t, uu, k], q_recv.at[c, u, xo],
                     chip(x, uu, v) + k,
                 )
 
-            send_far(d)
+            to(d)
 
             @pl.when(j != 2)
             def _():
-                send_far(c)
-
-        q_got[c, u, xo, vv] = q_part[xo, u, c, vv]
+                to(c)
+
+    def far_got(vv):
+        wide_got(xo, vv, c)
+        wide_got(xo, vv, d)
 
     senders = [(c, plus(u, n)) for n in (1, 2, 3)] + [(d, n) for n in range(4)]
     place = rem(y, 2) * 4 + x
@@ -305,34 +299,27 @@
         for n in range(1, 4):
             send(theirs, theirs, piece_send.at[g, n + 4], piece_recv.at[g, pair_place], row_chip(n, y) + c)
 
-    def add_q(xx):
+    def add_q(g, xx):
         for role, n in senders:
             got(q_got.at[role, n, xx], q_recv.at[role, n, xx])
 
         @pl.loop(0, 4)
         def _(zz):
             for yy in range(4):
-                q_out[zz, yy, xx] = (q_got[0, zz, xx, yy] + q_got[1, yy, xx, zz]).astype(jnp.bfloat16)
+                q_sum[xx, zz, yy] = (q_got[0, zz, xx, yy] + q_got[1, yy, xx, zz]).astype(jnp.bfloat16)
+
+        pltpu.make_async_copy(q_sum.at[xx], q_hbm.at[xx], q_left.at[g]).start()
 
     def share_kv(g, passed=True):
         for n in (1, 2, 3, 5, 6, 7) if passed else range(1, 8):
             there = (pair_place if n >= 4 else place) - x + plus(x, n)
             got(pieces.at[c, g, there], piece_recv.at[g, there])
         send(pieces.at[c, g], pieces.at[c, g], pair_send.at[g], pair_recv.at[g], mate)
-
-    def finish_kv():
-        for g in range(4):
-            got(pieces.at[d, g], pair_recv.at[g])
-
-        @pl.loop(0, 4)
-        def _(zz):
-            columns = pl.ds(pl.multiple_of(zz * 256, 256), 256)
-            for xx in range(4):
-                places = [((xx - n + 1) % 4, n) for n in range(8)]
-                wide_pieces = [pieces[k, g, n, :, columns].astype(jnp.float32) for g, n in places for k in (0, 1)]
-                for out, first in ((k_out, 0), (v_out, 8)):
-                    value = jnp.concatenate([w[first:first + 8] for w in wide_pieces], axis=0).T.astype(jnp.bfloat16)
-                    out[zz, :, xx] = value.reshape(4, 64, 128)
+        pltpu.make_async_copy(pieces.at[c, g], pieces_hbm.at[c, g], pieces_left.at[g, 0]).start()
+
+    def pair_got(g):
+        got(pieces.at[d, g], pair_recv.at[g])
+        pltpu.make_async_copy(pieces.at[d, g], pieces_hbm.at[d, g], pieces_left.at[g, 1]).start()
 
     load_wq.wait()
     for vv, k in ((vm, d), (vp, c), (vo, c), (vo, d)):
@@ -359,6 +346,12 @@
         q_block(x, plus(um, 2 * i))
         send_q(1, x, plus(2 * i, 3))
 
+    thin_got(xo, vm, d)
+    thin_got(xo, vp, c)
+    thin_got(xo, vo, c)
+    thin_got(xo, vo, d)
+    far_got(v)
+    far_rows(0, v, 1, 4)
     pass_x(vo)
     wkv_got(um, d)
     wkv_got(up, c)
@@ -391,24 +384,23 @@
         send_q(g, xx, 2)
         q_got[c, u, xx] = q_part[xx, u, c]
 
-    for vv, kk in ((vm, d), (vp, c), (vo, c), (vo, d)):
-        thin_got(xo, vv, kk)
-
-    @pl.loop(0, 3)
-    def _(t):
-        far_rows(t)
+    far_rows(0, v, 0, 1)
+
+    @pl.loop(0, 2)
+    def _(i):
+        far_got(plus(vm, 2 * i))
+        far_rows(1 + i, plus(vm, 2 * i), 0, 4)
 
     for g in range(3):
         add_kv(g, plus(xm, g))
-
-    @pl.loop(3, 4)
-    def _(t):
-        far_rows(t)
-
+    far_got(vo)
+    kv_group(3, xo)
+    far_rows(3, vo, 0, 4)
+    q_got[c, u, xo] = q_part[xo, u, c]
     for g in range(3):
         pass_kv(g)
     for g in range(3):
-        add_q(plus(xm, g))
+        add_q(g, plus(xm, g))
 
     got(other, row_send.at[0])
     for n, kind in enumerate(counts["kinds"]):
@@ -436,13 +428,49 @@
     add_kv(3, xo, direct=True)
     for g in range(3):
         share_kv(g)
-    add_q(xo)
+    add_q(3, xo)
     share_kv(3, passed=False)
-    finish_kv()
+    for g in range(4):
+        pair_got(g)
     for g in range(4):
         for n in (0, 1, 2, 3, 5, 6, 7):
             got(pieces.at[0, 0, 0], piece_send.at[g, n])
         got(pieces.at[0, 0], pair_send.at[g])
+        got(q_sum.at[0], q_left.at[g])
+        for n in (0, 1):
+            got(pieces.at[0, 0], pieces_left.at[g, n])
+
+
+def finish_kernel(q_hbm, pieces_hbm, q_out, k_out, v_out, q, pieces, k, v, loads, stores):
+    def lanes(zz):
+        return slice(zz * 256, (zz + 1) * 256)
+
+    piece_loads = [pltpu.make_async_copy(pieces_hbm.at[..., lanes(zz)], pieces.at[..., lanes(zz)], loads.at[zz]) for zz in range(4)]
+    q_loads = [pltpu.make_async_copy(q_hbm.at[xx], q.at[xx], loads.at[4 + xx]) for xx in range(4)]
+    for load in piece_loads + q_loads:
+        load.start()
+    copies = []
+
+    def store(src, dst):
+        copy = pltpu.make_async_copy(src, dst, stores.at[len(copies)])
+        copy.start()
+        copies.append(copy)
+
+    for zz in range(4):
+        piece_loads[zz].wait()
+        for xx in range(4):
+            places = [((xx - n + 1) % 4, n) for n in range(8)]
+            wide = [pieces[core, g, n, :, lanes(zz)].astype(jnp.float32) for g, n in places for core in (0, 1)]
+            for out, first in ((k, 0), (v, 8)):
+                value = jnp.concatenate([w[first:first + 8] for w in wide], axis=0).T.astype(jnp.bfloat16)
+                out[zz, :, xx] = value.reshape(4, 64, 128)
+        store(k.at[zz], k_out.at[zz])
+        store(v.at[zz], v_out.at[zz])
+    for xx in range(4):
+        q_loads[xx].wait()
+        store(q.at[xx], q_out.at[:, :, xx])
+    for copy in copies:
+        copy.wait()
 
 
 def solution(mesh):
@@ -453,11 +481,11 @@
         vmem = pl.BlockSpec(memory_space=pltpu.VMEM)
         bf16, f32 = jnp.bfloat16, jnp.float32
         out = jax.ShapeDtypeStruct((4, 4, 4, 64, 128), bf16)
-        outs = pl.pallas_call(
+        q_sum, pieces = pl.pallas_call(
             functools.partial(kernel, depth, half - half // 8),
-            out_shape=(out, out, out),
+            out_shape=(out, jax.ShapeDtypeStruct((2, 4, 8, 16, 1024), bf16)),
             in_specs=[any_space, vmem, any_space, any_space, any_space],
-            out_specs=(vmem, vmem, vmem),
+            out_specs=(any_space, any_space),
             scratch_shapes=[
                 pltpu.VMEM((32, depth), bf16),
                 pltpu.VMEM((32, half), bf16),
@@ -469,6 +497,7 @@
                 pltpu.VMEM((4, 4, 2, 16, 256), f32),
                 pltpu.VMEM((2, 4, 4, 4, 64, 128), f32),
                 pltpu.VMEM((2, 4, 4, 16, 256), f32),
+                pltpu.VMEM((4, 4, 4, 64, 128), bf16),
                 pltpu.VMEM((2, 4, 8, 16, 1024), bf16),
                 DMA((6,)),
                 DMA((4, 4, 2)),
@@ -487,9 +516,26 @@
                 DMA((4, 8)),
                 DMA((4,)),
                 DMA((4,)),
+                DMA((4,)),
+                DMA((4, 2)),
             ],
             compiler_params=pltpu.CompilerParams(collective_id=0, has_side_effects=True, vmem_limit_bytes=67043328),
         )(x_rows, norm_gain.reshape(1, depth), w_q.reshape(depth, 128), w_k.T, w_v.T)
+        outs = pl.pallas_call(
+            finish_kernel,
+            out_shape=(out, out, out),
+            in_specs=[any_space, any_space],
+            out_specs=(any_space, any_space, any_space),
+            scratch_shapes=[
+                pltpu.VMEM((4, 4, 4, 64, 128), bf16),
+                pltpu.VMEM((2, 4, 8, 16, 1024), bf16),
+                pltpu.VMEM((4, 4, 4, 64, 128), bf16),
+                pltpu.VMEM((4, 4, 4, 64, 128), bf16),
+                DMA((8,)),
+                DMA((12,)),
+            ],
+            compiler_params=pltpu.CompilerParams(vmem_limit_bytes=67043328),
+        )(q_sum, pieces)
         return tuple(value.reshape(4096, 1, 128) for value in outs)
 
     return jax.shard_map(

time: 161 us -> 157 us (0.975)
  local copies, waits for them, and re-layouts: 5.59 us -> 0 us
    unnamed x5 -> x0, local copies, waits for them, and re-layouts: 5.59 us -> none
    pallas_call x0 -> x1, Pallas kernels: none -> 3.19 us  [local_step(): pl.pallas_call(finish_kernel, out_shape=(out, out, out), in_specs=[any_sp...]
    pallas_call x1, Pallas kernels: 155 us -> 153 us  [local_step(): pl.pallas_call(functools.partial(kernel, depth, half - half // 8), out_sh...]
where the time goes in v6:
time: 157 us
  Pallas kernels  156 us (99%)
    pallas_call x1, Pallas kernels, local_step(): pl.pallas_call(functools.partial(kernel, depth, half - half // 8), out_sh...  153 us
    pallas_call x1, Pallas kernels, local_step(): pl.pallas_call(finish_kernel, out_shape=(out, out, out), in_specs=[any_sp...  3.19 us

profile of v6, /device:TPU:1, one launch (start us, length us, event | category | flops | bytes accessed | tf_op | source)
XLA Modules:
  0.0 156.9 jit_solution(11712145637982603084)
XLA Ops:
  0.6 153.1 %shard_map.76 = (bf16[4,4,4,64,128]{4,3,2,1,0:T(8,128)(2,1)}, bf16[2,4,8,16,1024]{4,3,2,1,0:T(8,128)(2,1)}) custom-call(bf16[32,16384]{1,0:T(8,128)(2,1)} %x_hbm.1, f32[1,16384]{1,0:T(1,128)} %bitcast.10, bf16[16384,128]{1,0:T(8,128)(2,1)} %bitcast.7, bf16[8,16384]{1,0:T(8,128)(2,1)} %bitcast.8, bf16[8,16384]{1,0:T(8,128)(2,1)} %bitcast.9), custom_call_target="tpu_custom_call" | custom-call | tf_op jit(solution)/shard_map/pallas_call | solution.py:484
  153.7 3.2 %shard_map.77 = (bf16[4,4,4,64,128]{4,3,2,1,0:T(8,128)(2,1)}, bf16[4,4,4,64,128]{4,3,2,1,0:T(8,128)(2,1)}, bf16[4,4,4,64,128]{4,3,2,1,0:T(8,128)(2,1)}) custom-call(bf16[4,4,4,64,128]{4,3,2,1,0:T(8,128)(2,1)} %get-tuple-element.8.q_hbm, bf16[2,4,8,16,1024]{4,3,2,1,0:T(8,128)(2,1)} %get-tuple-element.9.pieces_hbm), custom_call_target="tpu_custom_call" | custom-call | tf_op jit(solution)/shard_map/pallas_call | solution.py:524

commit v7 on v6

--- a/solution.py
+++ b/solution.py
@@ -19,7 +19,7 @@
 def kernel(
     depth, split, x_hbm, gain, wq_hbm, wk_hbm, wv_hbm, q_hbm, pieces_hbm,
     x_in, other, wkv_other, rows, wq, wkv, q_part, kv_part, q_got, kv_got, q_sum, pieces,
-    load_sem, wide_recv, thin_recv, row_send, wq_recv, wkv_recv, wq_send, wkv_send, q_send, q_send_far, kv_send, q_recv,
+    load_sem, wide_recv, thin_recv, row_send, wq_recv, wkv_recv, wq_send, wkv_send, q_send, kv_send, q_recv,
     kv_recv,
     piece_send, piece_recv, pair_send, pair_recv, q_left, pieces_left,
 ):
@@ -102,22 +102,20 @@
         load.wait()
     pl.semaphore_wait(barrier, len(peers))
 
-    counts = {"row": 0, "wq": 0, "wkv": 0, "kinds": []}
+    counts = {"wide": 0, "thin": 0, "wq": 0, "wkv": 0}
     wide, thin = slice(0, split), slice(split, half)
 
-    def row_sem():
-        counts["row"] += 1
-        return row_send.at[counts["row"] - 1]
+    def row_sem(kind):
+        counts[kind] += 1
+        return row_send.at[1 if counts[kind] <= 24 else 2]
 
     def send_wide(xx, vv, k, *to):
         for target in to:
-            send(rows.at[xx, vv, k, :, wide], rows.at[xx, vv, k, :, wide], row_sem(), wide_recv.at[xx, vv, k], target)
-            counts["kinds"].append(wide)
+            send(rows.at[xx, vv, k, :, wide], rows.at[xx, vv, k, :, wide], row_sem("wide"), wide_recv.at[xx, vv, k], target)
 
     def send_thin(xx, vv, k, *to):
         for target in to:
-            send(rows.at[xx, vv, k, :, thin], rows.at[xx, vv, k, :, thin], row_sem(), thin_recv.at[xx, vv, k], target)
-            counts["kinds"].append(thin)
+            send(rows.at[xx, vv, k, :, thin], rows.at[xx, vv, k, :, thin], row_sem("thin"), thin_recv.at[xx, vv, k], target)
 
     def wide_got(xx, vv, k):
         got(rows.at[xx, vv, k, :, wide], wide_recv.at[xx, vv, k])
@@ -126,11 +124,11 @@
         got(rows.at[xx, vv, k, :, thin], thin_recv.at[xx, vv, k])
 
     def send_wq(src, uu, k, target):
-        send(src, wq.at[uu, k], wq_send.at[counts["wq"]], wq_recv.at[uu, k], target)
+        send(src, wq.at[uu, k], wq_send.at[counts["wq"] // 6], wq_recv.at[uu, k], target)
         counts["wq"] += 1
 
     def send_wkv(src, uu, k, target):
-        send(src, wkv.at[uu, k], wkv_send.at[counts["wkv"]], wkv_recv.at[uu, k], target)
+        send(src, wkv.at[uu, k], wkv_send.at[counts["wkv"] // 6], wkv_recv.at[uu, k], target)
         counts["wkv"] += 1
 
     def wq_got(uu, k):
@@ -148,7 +146,7 @@
 
     near_x, near_v, near_u = (x_next, x_last), (v_next, v_last), (u_next, u_last)
 
-    send(other, rows.at[x, u, c], row_sem(), wide_recv.at[x, u, c], mate)
+    send(other, rows.at[x, u, c], row_send.at[0], wide_recv.at[x, u, c], mate)
     send_thin(x, v, c, *near_x)
     send_wide(x, v, c, *near_v)
     for target in near_u:
@@ -224,11 +222,12 @@
         for k in (0, 1):
             q_part[xx, uu, k] = value[:, k * 128:(k + 1) * 128].reshape(4, 64, 128)
 
-    def send_q(g, xx, du, whole=True):
+    def send_q(xx, du, whole=True):
         uu = plus(u, du)
 
         def to(k):
-            send(q_part.at[xx, uu, k], q_got.at[c, u, xx], q_send.at[g, du, k], q_recv.at[c, u, xx], chip(x, uu, v) + k)
+            mated = 1 - (du + 3) // 4
+            send(q_part.at[xx, uu, k], q_got.at[c, u, xx], q_send.at[mated], q_recv.at[c, xx], chip(x, uu, v) + k)
 
         to(d)
 
@@ -236,7 +235,7 @@
         def _():
             to(c)
 
-    def kv_group(g, xx):
+    def kv_group(xx):
         value = lax.dot_general(
             wkv[...].reshape(128, half), rows[xx].reshape(256, half), (((1,), (1,)), ((), ())), preferred_element_type=jnp.float32
         )
@@ -244,10 +243,10 @@
         for du in (2, 1, 3, 0):
             uu = plus(u, du)
             for k in ((c, d) if du else (d,)):
-                send(kv_part.at[xx, uu, k], kv_got.at[c, u, xx], kv_send.at[g, du, k], kv_recv.at[c, u, xx], chip(x, uu, v) + k)
+                send(kv_part.at[xx, uu, k], kv_got.at[c, u, xx], kv_send.at[0 if du else 1], kv_recv.at[c, xx], chip(x, uu, v) + k)
         kv_got[c, u, xx] = kv_part[xx, u, c]
 
-    def far_rows(t, vv, first, last):
+    def far_rows(vv, first, last, final=False):
         @pl.loop(first, last)
         def _(j):
             uu = plus(u, 2 + j)
@@ -255,38 +254,32 @@
             value = jnp.dot(rows[xo, vv].reshape(64, half), right, preferred_element_type=jnp.float32)
             for k in (0, 1):
                 q_part[xo, uu, k, vv] = value[:, k * 128:(k + 1) * 128]
-
-            def to(k):
-                send(
-                    q_part.at[xo, uu, k, vv], q_got.at[c, u, xo, vv], q_send_far.at[t, uu, k], q_recv.at[c, u, xo],
-                    chip(x, uu, v) + k,
-                )
-
-            to(d)
-
-            @pl.when(j != 2)
-            def _():
-                to(c)
+            if final:
+                send_q(xo, plus(j, 2), j != 2)
+
+                @pl.when(j == 1)
+                def _():
+                    for g in range(3):
+                        pass_kv(g)
 
     def far_got(vv):
         wide_got(xo, vv, c)
         wide_got(xo, vv, d)
 
-    senders = [(c, plus(u, n)) for n in (1, 2, 3)] + [(d, n) for n in range(4)]
     place = rem(y, 2) * 4 + x
 
     def add_kv(g, xx, direct=False):
-        for role, n in senders:
-            got(kv_got.at[role, n, xx], kv_recv.at[role, n, xx])
+        got(kv_got.at[0, 0:3, 0], kv_recv.at[c, xx])
+        got(kv_got.at[0, :, 0], kv_recv.at[d, xx])
         for zz in range(4):
             second = jnp.concatenate([kv_got[1, yy, xx][:, zz * 64:(zz + 1) * 64] for yy in range(4)], axis=1)
             pieces[c, g, place, :, pl.ds(zz * 256, 256)] = (kv_got[0, zz, xx] + second).astype(jnp.bfloat16)
         own = pieces.at[c, g, place]
+        send(own, own, piece_send, piece_recv.at[g, 0], row_chip(0, y_pair) + c)
         for n in range(1, 4):
-            send(own, own, piece_send.at[g, n], piece_recv.at[g, place], row_chip(n, y) + c)
+            send(own, own, piece_send, piece_recv.at[g, 1], row_chip(n, y) + c)
             if direct:
-                send(own, own, piece_send.at[g, n + 4], piece_recv.at[g, place], row_chip(n, y_pair) + c)
-        send(own, own, piece_send.at[g, 0], piece_recv.at[g, place], row_chip(0, y_pair) + c)
+                send(own, own, piece_send, piece_recv.at[g, 1], row_chip(n, y_pair) + c)
 
     def row_chip(n, yy):
         return ((z * 4 + yy) * 4 + plus(x, n)) * 2
@@ -294,32 +287,28 @@
     pair_place = 4 - place + 2 * x
 
     def pass_kv(g):
-        got(pieces.at[c, g, pair_place], piece_recv.at[g, pair_place])
         theirs = pieces.at[c, g, pair_place]
+        got(theirs, piece_recv.at[g, 0])
         for n in range(1, 4):
-            send(theirs, theirs, piece_send.at[g, n + 4], piece_recv.at[g, pair_place], row_chip(n, y) + c)
+            send(theirs, theirs, piece_send, piece_recv.at[g, 1], row_chip(n, y) + c)
 
     def add_q(g, xx):
-        for role, n in senders:
-            got(q_got.at[role, n, xx], q_recv.at[role, n, xx])
+        got(q_got.at[0, 0:3, 0], q_recv.at[c, xx])
+        got(q_got.at[0, :, 0], q_recv.at[d, xx])
 
         @pl.loop(0, 4)
         def _(zz):
             for yy in range(4):
                 q_sum[xx, zz, yy] = (q_got[0, zz, xx, yy] + q_got[1, yy, xx, zz]).astype(jnp.bfloat16)
 
-        pltpu.make_async_copy(q_sum.at[xx], q_hbm.at[xx], q_left.at[g]).start()
+        pltpu.make_async_copy(q_sum.at[xx], q_hbm.at[xx], q_left).start()
 
     def share_kv(g, passed=True):
-        for n in (1, 2, 3, 5, 6, 7) if passed else range(1, 8):
-            there = (pair_place if n >= 4 else place) - x + plus(x, n)
-            got(pieces.at[c, g, there], piece_recv.at[g, there])
-        send(pieces.at[c, g], pieces.at[c, g], pair_send.at[g], pair_recv.at[g], mate)
-        pltpu.make_async_copy(pieces.at[c, g], pieces_hbm.at[c, g], pieces_left.at[g, 0]).start()
-
-    def pair_got(g):
-        got(pieces.at[d, g], pair_recv.at[g])
-        pltpu.make_async_copy(pieces.at[d, g], pieces_hbm.at[d, g], pieces_left.at[g, 1]).start()
+        if not passed:
+            got(pieces.at[c, g, pair_place], piece_recv.at[g, 0])
+        got(pieces.at[c, g, 0:6], piece_recv.at[g, 1])
+        send(pieces.at[c, g], pieces.at[c, g], pair_send, pair_recv.at[g // 3], mate)
+        pltpu.make_async_copy(pieces.at[c, g], pieces_hbm.at[c, g], pieces_left).start()
 
     load_wq.wait()
     for vv, k in ((vm, d), (vp, c), (vo, c), (vo, d)):
@@ -328,7 +317,7 @@
     @pl.loop(0, 1)
     def _(i):
         q_block(x, plus(u, i))
-        send_q(1, x, 0, False)
+        send_q(x, 0, False)
 
     wq_got(um, c)
     send_wq(wq.at[um, c], um, c, u_next)
@@ -344,14 +333,14 @@
     @pl.loop(0, 2)
     def _(i):
         q_block(x, plus(um, 2 * i))
-        send_q(1, x, plus(2 * i, 3))
+        send_q(x, plus(2 * i, 3))
 
     thin_got(xo, vm, d)
     thin_got(xo, vp, c)
     thin_got(xo, vo, c)
     thin_got(xo, vo, d)
     far_got(v)
-    far_rows(0, v, 1, 4)
+    far_rows(v, 1, 4)
     pass_x(vo)
     wkv_got(um, d)
     wkv_got(up, c)
@@ -365,14 +354,14 @@
 
     @pl.loop(0, 3)
     def _(g):
-        kv_group(g, plus(xm, g))
+        kv_group(plus(xm, g))
 
     @pl.loop(0, 2)
     def _(i):
         @pl.loop(0, 3)
         def _(j):
             q_block(plus(xm, 2 * i), plus(um, j))
-            send_q(2 * i, plus(xm, 2 * i), plus(j, 3), j != 1)
+            send_q(plus(xm, 2 * i), plus(j, 3), j != 1)
 
     for k in (c, d):
         wq_got(uo, k)
@@ -381,64 +370,51 @@
     def _(g):
         xx = plus(xm, g)
         q_block(xx, uo)
-        send_q(g, xx, 2)
+        send_q(xx, 2)
         q_got[c, u, xx] = q_part[xx, u, c]
 
-    far_rows(0, v, 0, 1)
+    for g in range(3):
+        add_kv(g, plus(xm, g))
+    far_rows(v, 0, 1)
 
     @pl.loop(0, 2)
     def _(i):
         far_got(plus(vm, 2 * i))
-        far_rows(1 + i, plus(vm, 2 * i), 0, 4)
-
-    for g in range(3):
-        add_kv(g, plus(xm, g))
+        far_rows(plus(vm, 2 * i), 0, 4)
+
     far_got(vo)
-    kv_group(3, xo)
-    far_rows(3, vo, 0, 4)
+    kv_group(xo)
+    far_rows(vo, 0, 4, True)
     q_got[c, u, xo] = q_part[xo, u, c]
-    for g in range(3):
-        pass_kv(g)
+    add_kv(3, xo, direct=True)
     for g in range(3):
         add_q(g, plus(xm, g))
-
-    got(other, row_send.at[0])
-    for n, kind in enumerate(counts["kinds"]):
-        got(rows.at[0, 0, 0, :, kind], row_send.at[n + 1])
-    for n in range(counts["wq"]):
-        got(wq.at[0, 0], wq_send.at[n])
-    for n in range(counts["wkv"]):
-        got(wkv.at[0, 0], wkv_send.at[n])
-
-    @pl.loop(0, 4)
-    def _(du):
-        def drained(k):
-            for g in range(3):
-                got(q_part.at[0, 0, 0], q_send.at[g, du, k])
-            for t in range(4):
-                got(q_part.at[0, 0, 0, 0], q_send_far.at[t, plus(u, du), k])
-                got(kv_part.at[0, 0, 0], kv_send.at[t, du, k])
-
-        drained(d)
-
-        @pl.when(du > 0)
-        def _():
-            drained(c)
-
-    add_kv(3, xo, direct=True)
     for g in range(3):
         share_kv(g)
+
+    got(other, row_send.at[0])
+    got(rows.at[0:3], row_send.at[1])
+    got(rows.at[3, 0:3], row_send.at[2])
+    got(wq.at[0:3], wq_send.at[0])
+    got(wq.at[3, 0], wq_send.at[1])
+    got(wkv.at[0:3], wkv_send.at[0])
+    got(wkv.at[3, 0], wkv_send.at[1])
+    got(q_part.at[0:3], q_send.at[0])
+    got(q_part.at[3, 0:2], q_send.at[1])
+    got(kv_part.at[0:3], kv_send.at[0])
+    got(kv_part.at[3, 0:2], kv_send.at[1])
+
     add_q(3, xo)
+    got(pieces.at[d, 0:3], pair_recv.at[0])
+    for g in range(3):
+        pltpu.make_async_copy(pieces.at[d, g], pieces_hbm.at[d, g], pieces_left).start()
     share_kv(3, passed=False)
-    for g in range(4):
-        pair_got(g)
-    for g in range(4):
-        for n in (0, 1, 2, 3, 5, 6, 7):
-            got(pieces.at[0, 0, 0], piece_send.at[g, n])
-        got(pieces.at[0, 0], pair_send.at[g])
-        got(q_sum.at[0], q_left.at[g])
-        for n in (0, 1):
-            got(pieces.at[0, 0], pieces_left.at[g, n])
+    got(pieces.at[d, 3], pair_recv.at[1])
+    pltpu.make_async_copy(pieces.at[d, 3], pieces_hbm.at[d, 3], pieces_left).start()
+    got(pieces.at[0, :, 0:7], piece_send)
+    got(pieces.at[0], pair_send)
+    got(q_sum, q_left)
+    got(pieces, pieces_left)
 
 
 def finish_kernel(q_hbm, pieces_hbm, q_out, k_out, v_out, q, pieces, k, v, loads, stores):
@@ -482,7 +458,7 @@
         bf16, f32 = jnp.bfloat16, jnp.float32
         out = jax.ShapeDtypeStruct((4, 4, 4, 64, 128), bf16)
         q_sum, pieces = pl.pallas_call(
-            functools.partial(kernel, depth, half - half // 8),
+            functools.partial(kernel, depth, half - 5 * half // 32),
             out_shape=(out, jax.ShapeDtypeStruct((2, 4, 8, 16, 1024), bf16)),
             in_specs=[any_space, vmem, any_space, any_space, any_space],
             out_specs=(any_space, any_space),
@@ -502,22 +478,21 @@
                 DMA((6,)),
                 DMA((4, 4, 2)),
                 DMA((4, 4, 2)),
-                DMA((61,)),
+                DMA((3,)),
                 DMA((4, 2)),
                 DMA((4, 2)),
-                DMA((7,)),
-                DMA((7,)),
-                DMA((3, 4, 2)),
-                DMA((4, 4, 2)),
-                DMA((4, 4, 2)),
-                DMA((2, 4, 4)),
-                DMA((2, 4, 4)),
-                DMA((4, 8)),
-                DMA((4, 8)),
-                DMA((4,)),
-                DMA((4,)),
-                DMA((4,)),
+                DMA((2,)),
+                DMA((2,)),
+                DMA((2,)),
+                DMA((2,)),
+                DMA((2, 4)),
+                DMA((2, 4)),
+                DMA(()),
                 DMA((4, 2)),
+                DMA(()),
+                DMA((2,)),
+                DMA(()),
+                DMA(()),
             ],
             compiler_params=pltpu.CompilerParams(collective_id=0, has_side_effects=True, vmem_limit_bytes=67043328),
         )(x_rows, norm_gain.reshape(1, depth), w_q.reshape(depth, 128), w_k.T, w_v.T)

time: 157 us -> 149 us (0.949)
  Pallas kernels: 156 us -> 149 us
    pallas_call x1, Pallas kernels: 153 us -> 145 us  [local_step(): pl.pallas_call(functools.partial(kernel, depth, half - 5 * half // 32), o...]
where the time goes in v7:
time: 149 us
  Pallas kernels  149 us (100%)
    pallas_call x1, Pallas kernels, local_step(): pl.pallas_call(functools.partial(kernel, depth, half - 5 * half // 32), o...  145 us
    pallas_call x1, Pallas kernels, local_step(): pl.pallas_call(finish_kernel, out_shape=(out, out, out), in_specs=[any_sp...  3.19 us

profile of v7, /device:TPU:1, one launch (start us, length us, event | category | flops | bytes accessed | tf_op | source)
XLA Modules:
  0.0 149.3 jit_solution(7977658354230458612)
XLA Ops:
  0.6 145.4 %shard_map.76 = (bf16[4,4,4,64,128]{4,3,2,1,0:T(8,128)(2,1)}, bf16[2,4,8,16,1024]{4,3,2,1,0:T(8,128)(2,1)}) custom-call(bf16[32,16384]{1,0:T(8,128)(2,1)} %x_hbm.1, f32[1,16384]{1,0:T(1,128)} %bitcast.10, bf16[16384,128]{1,0:T(8,128)(2,1)} %bitcast.7, bf16[8,16384]{1,0:T(8,128)(2,1)} %bitcast.8, bf16[8,16384]{1,0:T(8,128)(2,1)} %bitcast.9), custom_call_target="tpu_custom_call" | custom-call | tf_op jit(solution)/shard_map/pallas_call | solution.py:460
  146.1 3.2 %shard_map.77 = (bf16[4,4,4,64,128]{4,3,2,1,0:T(8,128)(2,1)}, bf16[4,4,4,64,128]{4,3,2,1,0:T(8,128)(2,1)}, bf16[4,4,4,64,128]{4,3,2,1,0:T(8,128)(2,1)}) custom-call(bf16[4,4,4,64,128]{4,3,2,1,0:T(8,128)(2,1)} %get-tuple-element.8.q_hbm, bf16[2,4,8,16,1024]{4,3,2,1,0:T(8,128)(2,1)} %get-tuple-element.9.pieces_hbm), custom_call_target="tpu_custom_call" | custom-call | tf_op jit(solution)/shard_map/pallas_call | solution.py:499

commit v8 on v7

--- a/solution.py
+++ b/solution.py
@@ -17,9 +17,9 @@
 
 
 def kernel(
-    depth, split, x_hbm, gain, wq_hbm, wk_hbm, wv_hbm, q_hbm, pieces_hbm,
-    x_in, other, wkv_other, rows, wq, wkv, q_part, kv_part, q_got, kv_got, q_sum, pieces,
-    load_sem, wide_recv, thin_recv, row_send, wq_recv, wkv_recv, wq_send, wkv_send, q_send, kv_send, q_recv,
+    depth, split, middle, x_hbm, gain_hbm, wq_hbm, wk_hbm, wv_hbm, q_hbm, pieces_hbm,
+    x_in, gain, other, wkv_other, rows, wq, wkv, q_part, kv_part, q_got, kv_got, q_sum, pieces,
+    load_sem, wide_recv, late_recv, thin_recv, row_send, wq_recv, wkv_recv, wq_send, wkv_send, q_send, kv_send, q_recv,
     kv_recv,
     piece_send, piece_recv, pair_send, pair_recv, q_left, pieces_left,
 ):
@@ -53,6 +53,8 @@
 
     load_x = pltpu.make_async_copy(x_hbm, x_in, load_sem.at[0])
     load_x.start()
+    load_gain = pltpu.make_async_copy(gain_hbm, gain, load_sem.at[6])
+    load_gain.start()
     own_columns = pl.ds(pl.multiple_of(c * half, half), half)
     mate_columns = pl.ds(pl.multiple_of(d * half, half), half)
     loads = [
@@ -79,6 +81,7 @@
         pl.semaphore_signal(barrier, inc=1, device_id={"tp": peer}, device_id_type=MESH)
 
     load_x.wait()
+    load_gain.wait()
     width = min(1024, half)
 
     def squares(j, total):
@@ -104,6 +107,8 @@
 
     counts = {"wide": 0, "thin": 0, "wq": 0, "wkv": 0}
     wide, thin = slice(0, split), slice(split, half)
+    early, late, whole = slice(0, middle), slice(middle, split), slice(0, half)
+    rest = slice(middle, half)
 
     def row_sem(kind):
         counts[kind] += 1
@@ -116,6 +121,20 @@
     def send_thin(xx, vv, k, *to):
         for target in to:
             send(rows.at[xx, vv, k, :, thin], rows.at[xx, vv, k, :, thin], row_sem("thin"), thin_recv.at[xx, vv, k], target)
+
+    def send_early(xx, k, *to):
+        for target in to:
+            send(rows.at[xx, vo, k, :, early], rows.at[xx, vo, k, :, early], row_send.at[2], wide_recv.at[xx, vo, k], target)
+
+    def send_late(xx, k, *to):
+        for target in to:
+            send(rows.at[xx, vo, k, :, late], rows.at[xx, vo, k, :, late], row_send.at[2], late_recv.at[xx, k], target)
+
+    def early_got(xx, k):
+        got(rows.at[xx, vo, k, :, early], wide_recv.at[xx, vo, k])
+
+    def late_got(xx, k):
+        got(rows.at[xx, vo, k, :, late], late_recv.at[xx, k])
 
     def wide_got(xx, vv, k):
         got(rows.at[xx, vv, k, :, wide], wide_recv.at[xx, vv, k])
@@ -209,7 +228,8 @@
         send_thin(xo, v, k, *near_v)
     for k in (c, d):
         wide_got(x, vo, k)
-        send_wide(x, vo, k, *near_x)
+        send_early(x, k, *near_x)
+        send_late(x, k, *near_x)
     for xx in (x, xm, xp, xo):
         thin_got(xx, vm, c)
         send_thin(xx, vm, c, v_next)
@@ -235,26 +255,34 @@
         def _():
             to(c)
 
-    def kv_group(xx):
+    def kv_value(xx, columns):
+        count = columns.stop - columns.start
         value = lax.dot_general(
-            wkv[...].reshape(128, half), rows[xx].reshape(256, half), (((1,), (1,)), ((), ())), preferred_element_type=jnp.float32
+            wkv[:, :, :, columns].reshape(128, count), rows[xx, :, :, :, columns].reshape(256, count),
+            (((1,), (1,)), ((), ())), preferred_element_type=jnp.float32,
         )
-        kv_part[xx] = value.reshape(4, 2, 16, 256)
+        return value.reshape(4, 2, 16, 256)
+
+    def send_kv(xx):
         for du in (2, 1, 3, 0):
             uu = plus(u, du)
             for k in ((c, d) if du else (d,)):
                 send(kv_part.at[xx, uu, k], kv_got.at[c, u, xx], kv_send.at[0 if du else 1], kv_recv.at[c, xx], chip(x, uu, v) + k)
         kv_got[c, u, xx] = kv_part[xx, u, c]
 
-    def far_rows(vv, first, last, final=False):
+    def far_rows(vv, first, last, columns, second=False):
+        count = columns.stop - columns.start
+
         @pl.loop(first, last)
         def _(j):
             uu = plus(u, 2 + j)
-            right = jnp.concatenate([wq[uu, 0], wq[uu, 1]], axis=1)
-            value = jnp.dot(rows[xo, vv].reshape(64, half), right, preferred_element_type=jnp.float32)
+            right = jnp.concatenate([wq[uu, 0, columns], wq[uu, 1, columns]], axis=1)
+            left = rows[xo, vv, :, :, columns].reshape(64, count)
+            value = jnp.dot(left, right, preferred_element_type=jnp.float32)
             for k in (0, 1):
-                q_part[xo, uu, k, vv] = value[:, k * 128:(k + 1) * 128]
-            if final:
+                part = value[:, k * 128:(k + 1) * 128]
+                q_part[xo, uu, k, vv] = q_part[xo, uu, k, vv] + part if second else part
+            if second:
                 send_q(xo, plus(j, 2), j != 2)
 
                 @pl.when(j == 1)
@@ -340,21 +368,29 @@
     thin_got(xo, vo, c)
     thin_got(xo, vo, d)
     far_got(v)
-    far_rows(v, 1, 4)
-    pass_x(vo)
+    far_rows(v, 1, 4, whole)
+    for xx, k, target in ((xm, c, x_next), (xp, d, x_last)):
+        early_got(xx, k)
+        send_early(xx, k, target)
+        late_got(xx, k)
+        send_late(xx, k, target)
     wkv_got(um, d)
     wkv_got(up, c)
     for k in (c, d):
         wkv_got(uo, k)
     for xx, k in ((xm, d), (xp, c)):
-        for vv in (v, vm, vp, vo):
+        for vv in (v, vm, vp):
             wide_got(xx, vv, k)
+        early_got(xx, k)
+        late_got(xx, k)
         for vv, kk in ((vm, d), (vp, c), (vo, c), (vo, d)):
             thin_got(xx, vv, kk)
 
     @pl.loop(0, 3)
     def _(g):
-        kv_group(plus(xm, g))
+        xx = plus(xm, g)
+        kv_part[xx] = kv_value(xx, slice(0, half))
+        send_kv(xx)
 
     @pl.loop(0, 2)
     def _(i):
@@ -375,22 +411,33 @@
 
     for g in range(3):
         add_kv(g, plus(xm, g))
-    far_rows(v, 0, 1)
+    far_rows(v, 0, 1, whole)
 
     @pl.loop(0, 2)
     def _(i):
         far_got(plus(vm, 2 * i))
-        far_rows(plus(vm, 2 * i), 0, 4)
-
-    far_got(vo)
-    kv_group(xo)
-    far_rows(vo, 0, 4, True)
+        far_rows(plus(vm, 2 * i), 0, 4, whole)
+
+    for k in (c, d):
+        early_got(xo, k)
+    kv_part[xo] = kv_value(xo, early)
+    far_rows(vo, 0, 4, early)
+    for k in (c, d):
+        late_got(xo, k)
+    kv_part[xo] = kv_part[xo] + kv_value(xo, rest)
+    send_kv(xo)
+    far_rows(vo, 0, 4, rest, True)
     q_got[c, u, xo] = q_part[xo, u, c]
     add_kv(3, xo, direct=True)
     for g in range(3):
         add_q(g, plus(xm, g))
     for g in range(3):
         share_kv(g)
+
+    got(pieces.at[d, 0:3], pair_recv.at[0])
+    for g in range(3):
+        pltpu.make_async_copy(pieces.at[d, g], pieces_hbm.at[d, g], pieces_left).start()
+    share_kv(3, passed=False)
 
     got(other, row_send.at[0])
     got(rows.at[0:3], row_send.at[1])
@@ -399,18 +446,14 @@
     got(wq.at[3, 0], wq_send.at[1])
     got(wkv.at[0:3], wkv_send.at[0])
     got(wkv.at[3, 0], wkv_send.at[1])
+    got(kv_part.at[0:3], kv_send.at[0])
+    got(kv_part.at[3, 0:2], kv_send.at[1])
+
+    got(pieces.at[d, 3], pair_recv.at[1])
+    pltpu.make_async_copy(pieces.at[d, 3], pieces_hbm.at[d, 3], pieces_left).start()
+    add_q(3, xo)
     got(q_part.at[0:3], q_send.at[0])
     got(q_part.at[3, 0:2], q_send.at[1])
-    got(kv_part.at[0:3], kv_send.at[0])
-    got(kv_part.at[3, 0:2], kv_send.at[1])
-
-    add_q(3, xo)
-    got(pieces.at[d, 0:3], pair_recv.at[0])
-    for g in range(3):
-        pltpu.make_async_copy(pieces.at[d, g], pieces_hbm.at[d, g], pieces_left).start()
-    share_kv(3, passed=False)
-    got(pieces.at[d, 3], pair_recv.at[1])
-    pltpu.make_async_copy(pieces.at[d, 3], pieces_hbm.at[d, 3], pieces_left).start()
     got(pieces.at[0, :, 0:7], piece_send)
     got(pieces.at[0], pair_send)
     got(q_sum, q_left)
@@ -454,16 +497,16 @@
         depth = x_rows.shape[1]
         half = depth // 2
         any_space = pl.BlockSpec(memory_space=pl.ANY)
-        vmem = pl.BlockSpec(memory_space=pltpu.VMEM)
         bf16, f32 = jnp.bfloat16, jnp.float32
         out = jax.ShapeDtypeStruct((4, 4, 4, 64, 128), bf16)
         q_sum, pieces = pl.pallas_call(
-            functools.partial(kernel, depth, half - 5 * half // 32),
+            functools.partial(kernel, depth, half - 5 * half // 32, 17 * half // 32),
             out_shape=(out, jax.ShapeDtypeStruct((2, 4, 8, 16, 1024), bf16)),
-            in_specs=[any_space, vmem, any_space, any_space, any_space],
+            in_specs=[any_space] * 5,
             out_specs=(any_space, any_space),
             scratch_shapes=[
                 pltpu.VMEM((32, depth), bf16),
+                pltpu.VMEM((1, depth), f32),
                 pltpu.VMEM((32, half), bf16),
                 pltpu.VMEM((16, half), bf16),
                 pltpu.VMEM((4, 4, 2, 32, half), bf16),
@@ -475,8 +518,9 @@
                 pltpu.VMEM((2, 4, 4, 16, 256), f32),
                 pltpu.VMEM((4, 4, 4, 64, 128), bf16),
                 pltpu.VMEM((2, 4, 8, 16, 1024), bf16),
-                DMA((6,)),
+                DMA((7,)),
                 DMA((4, 4, 2)),
+                DMA((4, 2)),
                 DMA((4, 4, 2)),
                 DMA((3,)),
                 DMA((4, 2)),

time: 149 us -> 148 us (level)
  Pallas kernels: 149 us -> 147 us
where the time goes in v8:
time: 148 us
  Pallas kernels  147 us (99%)
    pallas_call x1, Pallas kernels, local_step(): pl.pallas_call(functools.partial(kernel, depth, half - 5 * half // 32, 17...  144 us
    pallas_call x1, Pallas kernels, local_step(): pl.pallas_call(finish_kernel, out_shape=(out, out, out), in_specs=[any_sp...  3.19 us

profile of v8, /device:TPU:1, one launch (start us, length us, event | category | flops | bytes accessed | tf_op | source)
XLA Modules:
  0.0 147.8 jit_solution(13723923370982280540)
XLA Ops:
  0.6 144.0 %shard_map.76 = (bf16[4,4,4,64,128]{4,3,2,1,0:T(8,128)(2,1)}, bf16[2,4,8,16,1024]{4,3,2,1,0:T(8,128)(2,1)}) custom-call(bf16[32,16384]{1,0:T(8,128)(2,1)} %x_hbm.1, f32[1,16384]{1,0:T(1,128)} %bitcast.10, bf16[16384,128]{1,0:T(8,128)(2,1)} %bitcast.7, bf16[8,16384]{1,0:T(8,128)(2,1)} %bitcast.8, bf16[8,16384]{1,0:T(8,128)(2,1)} %bitcast.9), custom_call_target="tpu_custom_call" | custom-call | tf_op jit(solution)/shard_map/pallas_call | solution.py:502
  144.6 3.2 %shard_map.77 = (bf16[4,4,4,64,128]{4,3,2,1,0:T(8,128)(2,1)}, bf16[4,4,4,64,128]{4,3,2,1,0:T(8,128)(2,1)}, bf16[4,4,4,64,128]{4,3,2,1,0:T(8,128)(2,1)}) custom-call(bf16[4,4,4,64,128]{4,3,2,1,0:T(8,128)(2,1)} %get-tuple-element.8.q_hbm, bf16[2,4,8,16,1024]{4,3,2,1,0:T(8,128)(2,1)} %get-tuple-element.9.pieces_hbm), custom_call_target="tpu_custom_call" | custom-call | tf_op jit(solution)/shard_map/pallas_call | solution.py:543

commit v9 on v8

--- a/solution.py
+++ b/solution.py
@@ -288,7 +288,9 @@
                 @pl.when(j == 1)
                 def _():
                     for g in range(3):
-                        pass_kv(g)
+                        pass_on(g, pair_row + x, 0, (ahead, 3), (behind, 1))
+                    for g in range(3):
+                        pass_on(g, row_place + x_behind, 2, (ahead, 1))
 
     def far_got(vv):
         wide_got(xo, vv, c)
@@ -303,22 +305,28 @@
             second = jnp.concatenate([kv_got[1, yy, xx][:, zz * 64:(zz + 1) * 64] for yy in range(4)], axis=1)
             pieces[c, g, place, :, pl.ds(zz * 256, 256)] = (kv_got[0, zz, xx] + second).astype(jnp.bfloat16)
         own = pieces.at[c, g, place]
-        send(own, own, piece_send, piece_recv.at[g, 0], row_chip(0, y_pair) + c)
-        for n in range(1, 4):
-            send(own, own, piece_send, piece_recv.at[g, 1], row_chip(n, y) + c)
-            if direct:
-                send(own, own, piece_send, piece_recv.at[g, 1], row_chip(n, y_pair) + c)
-
-    def row_chip(n, yy):
-        return ((z * 4 + yy) * 4 + plus(x, n)) * 2
-
-    pair_place = 4 - place + 2 * x
-
-    def pass_kv(g):
-        theirs = pieces.at[c, g, pair_place]
-        got(theirs, piece_recv.at[g, 0])
-        for n in range(1, 4):
-            send(theirs, theirs, piece_send, piece_recv.at[g, 1], row_chip(n, y) + c)
+        send(own, own, piece_send, piece_recv.at[g, 0], across)
+        if direct:
+            for n in range(1, 4):
+                send(own, own, piece_send, piece_recv.at[g, 1], row_chip(plus(x, n), y) + c)
+                send(own, own, piece_send, piece_recv.at[g, 1], row_chip(plus(x, n), y_pair) + c)
+        else:
+            send(own, own, piece_send, piece_recv.at[g, 2], ahead)
+            send(own, own, piece_send, piece_recv.at[g, 1], behind)
+
+    def row_chip(xx, yy):
+        return ((z * 4 + yy) * 4 + xx) * 2
+
+    x_behind = plus(x, 3 - 2 * c)
+    ahead, behind = row_chip(plus(x, 1 + 2 * c), y) + c, row_chip(x_behind, y) + c
+    across = row_chip(x, y_pair) + c
+    row_place, pair_row = place - x, 4 - place + x
+
+    def pass_on(g, there, came, *to):
+        theirs = pieces.at[c, g, there]
+        got(theirs, piece_recv.at[g, came])
+        for target, lands in to:
+            send(theirs, theirs, piece_send, piece_recv.at[g, lands], target)
 
     def add_q(g, xx):
         got(q_got.at[0, 0:3, 0], q_recv.at[c, xx])
@@ -333,8 +341,8 @@
 
     def share_kv(g, passed=True):
         if not passed:
-            got(pieces.at[c, g, pair_place], piece_recv.at[g, 0])
-        got(pieces.at[c, g, 0:6], piece_recv.at[g, 1])
+            got(pieces.at[c, g, pair_row + x], piece_recv.at[g, 0])
+        got(pieces.at[c, g, 0:4 if passed else 6], piece_recv.at[g, 1])
         send(pieces.at[c, g], pieces.at[c, g], pair_send, pair_recv.at[g // 3], mate)
         pltpu.make_async_copy(pieces.at[c, g], pieces_hbm.at[c, g], pieces_left).start()
 
@@ -429,6 +437,8 @@
     far_rows(vo, 0, 4, rest, True)
     q_got[c, u, xo] = q_part[xo, u, c]
     add_kv(3, xo, direct=True)
+    for g in range(3):
+        pass_on(g, pair_row + x_behind, 3, (ahead, 1))
     for g in range(3):
         add_q(g, plus(xm, g))
     for g in range(3):
@@ -500,7 +510,7 @@
         bf16, f32 = jnp.bfloat16, jnp.float32
         out = jax.ShapeDtypeStruct((4, 4, 4, 64, 128), bf16)
         q_sum, pieces = pl.pallas_call(
-            functools.partial(kernel, depth, half - 5 * half // 32, 17 * half // 32),
+            functools.partial(kernel, depth, half - 11 * half // 64, 17 * half // 32),
             out_shape=(out, jax.ShapeDtypeStruct((2, 4, 8, 16, 1024), bf16)),
             in_specs=[any_space] * 5,
             out_specs=(any_space, any_space),
@@ -532,7 +542,7 @@
                 DMA((2, 4)),
                 DMA((2, 4)),
                 DMA(()),
-                DMA((4, 2)),
+                DMA((4, 4)),
                 DMA(()),
                 DMA((2,)),
                 DMA(()),

time: 148 us -> 148 us (level)
  no operation moved by 1% of the time
where the time goes in v9:
time: 148 us; the launch traced here: 147 us
  Pallas kernels  147 us (99%)
    pallas_call x1, Pallas kernels, local_step(): pl.pallas_call(functools.partial(kernel, depth, half - 11 * half // 64, 1...  144 us
    pallas_call x1, Pallas kernels, local_step(): pl.pallas_call(finish_kernel, out_shape=(out, out, out), in_specs=[any_sp...  3.19 us

profile of v9, /device:TPU:1, one launch (start us, length us, event | category | flops | bytes accessed | tf_op | source)
XLA Modules:
  0.0 147.5 jit_solution(12216667371348646548)
XLA Ops:
  0.6 143.6 %shard_map.76 = (bf16[4,4,4,64,128]{4,3,2,1,0:T(8,128)(2,1)}, bf16[2,4,8,16,1024]{4,3,2,1,0:T(8,128)(2,1)}) custom-call(bf16[32,16384]{1,0:T(8,128)(2,1)} %x_hbm.1, f32[1,16384]{1,0:T(1,128)} %bitcast.10, bf16[16384,128]{1,0:T(8,128)(2,1)} %bitcast.7, bf16[8,16384]{1,0:T(8,128)(2,1)} %bitcast.8, bf16[8,16384]{1,0:T(8,128)(2,1)} %bitcast.9), custom_call_target="tpu_custom_call" | custom-call | tf_op jit(solution)/shard_map/pallas_call | solution.py:512
  144.3 3.2 %shard_map.77 = (bf16[4,4,4,64,128]{4,3,2,1,0:T(8,128)(2,1)}, bf16[4,4,4,64,128]{4,3,2,1,0:T(8,128)(2,1)}, bf16[4,4,4,64,128]{4,3,2,1,0:T(8,128)(2,1)}) custom-call(bf16[4,4,4,64,128]{4,3,2,1,0:T(8,128)(2,1)} %get-tuple-element.8.q_hbm, bf16[2,4,8,16,1024]{4,3,2,1,0:T(8,128)(2,1)} %get-tuple-element.9.pieces_hbm), custom_call_target="tpu_custom_call" | custom-call | tf_op jit(solution)/shard_map/pallas_call | solution.py:553

commit v10 on v9

--- a/solution.py
+++ b/solution.py
@@ -444,10 +444,13 @@
     for g in range(3):
         share_kv(g)
 
+    share_kv(3, passed=False)
+    add_q(3, xo)
     got(pieces.at[d, 0:3], pair_recv.at[0])
     for g in range(3):
         pltpu.make_async_copy(pieces.at[d, g], pieces_hbm.at[d, g], pieces_left).start()
-    share_kv(3, passed=False)
+    got(pieces.at[d, 3], pair_recv.at[1])
+    pltpu.make_async_copy(pieces.at[d, 3], pieces_hbm.at[d, 3], pieces_left).start()
 
     got(other, row_send.at[0])
     got(rows.at[0:3], row_send.at[1])
@@ -459,9 +462,6 @@
     got(kv_part.at[0:3], kv_send.at[0])
     got(kv_part.at[3, 0:2], kv_send.at[1])
 
-    got(pieces.at[d, 3], pair_recv.at[1])
-    pltpu.make_async_copy(pieces.at[d, 3], pieces_hbm.at[d, 3], pieces_left).start()
-    add_q(3, xo)
     got(q_part.at[0:3], q_send.at[0])
     got(q_part.at[3, 0:2], q_send.at[1])
     got(pieces.at[0, :, 0:7], piece_send)

time: 148 us -> 147 us (level)
  no operation moved by 1% of the time
where the time goes in v10:
time: 147 us
  Pallas kernels  147 us (100%)
    pallas_call x1, Pallas kernels, local_step(): pl.pallas_call(functools.partial(kernel, depth, half - 11 * half // 64, 1...  144 us
    pallas_call x1, Pallas kernels, local_step(): pl.pallas_call(finish_kernel, out_shape=(out, out, out), in_specs=[any_sp...  3.19 us

profile of v10, /device:TPU:1, one launch (start us, length us, event | category | flops | bytes accessed | tf_op | source)
XLA Modules:
  0.0 147.3 jit_solution(9424635025564205315)
XLA Ops:
  0.6 143.5 %shard_map.76 = (bf16[4,4,4,64,128]{4,3,2,1,0:T(8,128)(2,1)}, bf16[2,4,8,16,1024]{4,3,2,1,0:T(8,128)(2,1)}) custom-call(bf16[32,16384]{1,0:T(8,128)(2,1)} %x_hbm.1, f32[1,16384]{1,0:T(1,128)} %bitcast.10, bf16[16384,128]{1,0:T(8,128)(2,1)} %bitcast.7, bf16[8,16384]{1,0:T(8,128)(2,1)} %bitcast.8, bf16[8,16384]{1,0:T(8,128)(2,1)} %bitcast.9), custom_call_target="tpu_custom_call" | custom-call | tf_op jit(solution)/shard_map/pallas_call | solution.py:512
  144.2 3.2 %shard_map.77 = (bf16[4,4,4,64,128]{4,3,2,1,0:T(8,128)(2,1)}, bf16[4,4,4,64,128]{4,3,2,1,0:T(8,128)(2,1)}, bf16[4,4,4,64,128]{4,3,2,1,0:T(8,128)(2,1)}) custom-call(bf16[4,4,4,64,128]{4,3,2,1,0:T(8,128)(2,1)} %get-tuple-element.8.q_hbm, bf16[2,4,8,16,1024]{4,3,2,1,0:T(8,128)(2,1)} %get-tuple-element.9.pieces_hbm), custom_call_target="tpu_custom_call" | custom-call | tf_op jit(solution)/shard_map/pallas_call | solution.py:553
